TPU v7x, 128 devices: a whole 4x4x4 slice. The times are simulated.
128 devices in a mesh: dp: 1, tp: 128 (over z, y, x, core).
Axes of the slice: x: 4, y: 4, z: 4, core: 2. Of those that a mesh axis runs over, the one named last changes fastest.
Arguments:
- queries: bfloat16 [2048, 768], P(('dp', 'tp'))
- w_first: bfloat16 [768, 768], replicated
- w_second: bfloat16 [768, 128], replicated
- catalogue: bfloat16 [1048576, 128], P('tp')
- log_q: float32 [1048576], P('tp')
- labels: int32 [2048], P(('dp', 'tp'))
Outputs:
- output 1: float32 [1], P('dp')
- output 2: bfloat16 [1048576, 128], P(('dp', 'tp'))
- output 3: bfloat16 [768, 768], P('dp')
- output 4: bfloat16 [768, 128], P('dp')
All inputs are finite; a program needn't handle non-finite values.
Results may differ from a plain program's by a relative error of at most 0.00441204.
Values are sent between devices in bfloat16 or wider.
A program may use at most 1 GiB of HBM per device.

v0:
```python
import jax
import jax.numpy as jnp
from jax import lax
from jax.sharding import PartitionSpec as P


def solution(mesh):
    def local_step(queries, w_first, w_second, catalogue, log_q, labels):
        items_local = catalogue.shape[0]
        shard_index = lax.axis_index("tp")
        pre_act = jnp.dot(queries, w_first, preferred_element_type=jnp.float32)
        hidden = jnp.maximum(pre_act, 0.0).astype(jnp.bfloat16)
        query_emb = jnp.dot(hidden, w_second, preferred_element_type=jnp.float32).astype(jnp.bfloat16)
        emb_all = lax.all_gather(query_emb, "tp", axis=0, tiled=True)
        labels_all = lax.all_gather(labels, "tp", axis=0, tiled=True)
        total_rows = emb_all.shape[0]
        logits = lax.dot_general(emb_all, catalogue, (((1,), (1,)), ((), ())), preferred_element_type=jnp.float32) - log_q[None, :]
        local_max = jnp.max(logits, axis=1)
        local_ids = labels_all - shard_index * items_local
        label_hit = lax.broadcasted_iota(jnp.int32, (1, items_local), 1) == local_ids[:, None]
        local_target = jnp.sum(jnp.where(label_hit, logits, 0.0), axis=1)
        exp_local = jnp.exp(logits - local_max[:, None])
        local_sum = jnp.sum(exp_local, axis=1)
        row_max = lax.pmax(local_max, "tp")
        rescale = jnp.exp(local_max - row_max)
        row_stats = lax.psum(jnp.stack([local_sum * rescale, local_target]), "tp")
        sum_exp = row_stats[0]
        mean_loss = jnp.mean(row_max + jnp.log(sum_exp) - row_stats[1]).reshape(1)
        soft_prob = exp_local * (rescale / sum_exp)[:, None]
        grad_logits = (jnp.where(label_hit, soft_prob - 1.0, soft_prob) / total_rows).astype(jnp.bfloat16)
        grad_items = lax.dot_general(grad_logits, emb_all, (((0,), (0,)), ((), ())), preferred_element_type=jnp.float32).astype(jnp.bfloat16)
        emb_part = jnp.dot(grad_logits, catalogue, preferred_element_type=jnp.float32)
        grad_emb = lax.psum_scatter(emb_part, "tp", scatter_dimension=0, tiled=True).astype(jnp.bfloat16)
        second_part = lax.dot_general(hidden, grad_emb, (((0,), (0,)), ((), ())), preferred_element_type=jnp.float32)
        grad_hidden = lax.dot_general(grad_emb, w_second, (((1,), (1,)), ((), ())), preferred_element_type=jnp.float32)
        grad_pre = jnp.where(pre_act > 0.0, grad_hidden, 0.0).astype(jnp.bfloat16)
        first_part = lax.dot_general(queries, grad_pre, (((0,), (0,)), ((), ())), preferred_element_type=jnp.float32)
        grad_first, grad_second = lax.psum((first_part, second_part), "tp")
        return mean_loss, grad_items, grad_first.astype(jnp.bfloat16), grad_second.astype(jnp.bfloat16)

    row_spec = P(("dp", "tp"), None)
    return jax.shard_map(local_step, mesh=mesh, in_specs=(row_spec, P(None, None), P(None, None), P("tp", None), P("tp"), P(("dp", "tp"))), out_specs=(P("dp"), row_spec, P("dp", None), P("dp", None)), check_vma=False)
```

profile of v0, /device:TPU:1, one launch (start us, length us, event | category | flops | bytes accessed | tf_op | source)
XLA Modules:
  0.0 1094.7 jit_solution(5848366959551597617)
XLA Ops:
  7.2 0.0 copy-start
  7.2 0.0 copy-start.1
  7.2 0.0 reduce-scatter.2.cloned.1.call-start
  7.3 1.0 dynamic-update-slice
  8.2 68.7 %all-reduce = s32[2048]{0:T(1024)S(1)} all-reduce(s32[2048]{0:T(1024)S(1)} %dynamic-update-slice), channel_id=1, replica_groups=mesh['dp'=1,'tp'=128] {'tp'}, use_global_device_ids=true, to_apply=%add | all-reduce | flops 2048 | bytes 16384
  76.9 1.6 fusion.16
  78.5 1.1 convolution_convert_fusion.1
  79.6 34.5 %all_gather.6 = bf16[2048,128]{1,0:T(8,128)(2,1)S(1)} all-gather(bf16[16,128]{1,0:T(8,128)(2,1)S(1)} %convolution_convert_fusion.1), channel_id=1, replica_groups=mesh['dp'=1,'tp'=128] {'tp'}, dimensions={0}, use_global_device_ids=true | all-gather | bytes 528384 | tf_op jit(solution)/shard_map/all_gather | solution.py:14
  114.1 0.0 copy-done
  114.1 23.8 %subtract_reduce_fusion = (f32[2048]{0:T(1024)S(1)}, f32[2048,8192]{1,0:T(8,128)}) fusion(f32[8192]{0:T(1024)} %param.10, bf16[2048,128]{1,0:T(8,128)(2,1)S(1)} %all_gather.6, bf16[8192,128]{1,0:T(8,128)(2,1)S(1)} %copy-done), kind=kOutput, calls=%fused_computation.7 | convolution fusion | flops 4328519680 | bytes 69771264 | tf_op jit(solution)/shard_map/dot_general | solution.py:17
  137.8 62.1 %pmax.7 = f32[2048]{0:T(1024)S(1)} all-reduce(f32[2048]{0:T(1024)S(1)} %get-tuple-element.16), channel_id=1, replica_groups=mesh['dp'=1,'tp'=128] {'tp'}, use_global_device_ids=true, to_apply=%region_1.2 | all-reduce | flops 2048 | bytes 16384 | tf_op jit(solution)/shard_map/pmax | solution.py:24
  199.9 0.0 copy-done.1
  199.9 25.0 %fusion.2 = (f32[2048]{0:T(1024)S(1)}, f32[2048]{0:T(1024)S(1)}) fusion(f32[2048,8192]{1,0:T(8,128)} %get-tuple-element.17, f32[2048]{0:T(1024)S(1)} %get-tuple-element.16, f32[8192]{0:T(1024)S(1)} %copy-done.1, s32[2048]{0:T(1024)S(1)} %broadcast_subtract_fusion), kind=kLoop, calls=%fused_computation.6 | loop fusion | flops 100659200 | bytes 67174400 | tf_op jit(solution)/shard_map/reduce_sum | solution.py:23
  225.0 64.3 %psum.21 = f32[2,2048]{1,0:T(2,128)S(1)} all-reduce(f32[2,2048]{1,0:T(2,128)S(1)} %pad_maximum_fusion), channel_id=1, replica_groups=mesh['dp'=1,'tp'=128] {'tp'}, use_global_device_ids=true, to_apply=%region_4.5 | all-reduce | flops 4096 | bytes 32768 | tf_op jit(solution)/shard_map/psum | solution.py:26
  289.3 0.6 fusion.7
  289.9 33.7 %fusion.1 = bf16[2048,8192]{1,0:T(8,128)(2,1)} fusion(f32[2048,8192]{1,0:T(8,128)} %get-tuple-element.17, f32[2048]{0:T(1024)S(1)} %get-tuple-element.12, s32[2048]{0:T(1024)S(1)} %broadcast_subtract_fusion, f32[2048]{0:T(1024)S(1)} %get-tuple-element.16, f32[8192]{0:T(1024)S(1)} %copy-done.1), kind=kLoop, calls=%fused_computation.2 | loop fusion | flops 134217728 | bytes 100720640 | tf_op jit(solution)/shard_map/convert_element_type | solution.py:30
  323.6 0.0 copy-start.2
  323.6 0.0 copy-start.3
  323.6 16.1 %fusion.17 = f32[2048,128]{1,0:T(8,128)} fusion(bf16[2048,8192]{1,0:T(8,128)(2,1)} %fusion.1, bf16[8192,128]{1,0:T(8,128)(2,1)S(1)} %copy-done), kind=kOutput, calls=%fused_computation.30 | convolution fusion | flops 4294967296 | bytes 36700160 | tf_op jit(solution)/shard_map/dot_general | solution.py:32
  339.7 0.0 reduce-scatter.2.cloned.1.call-update
  340.3 16.6 %convolution_convert_fusion = bf16[8192,128]{1,0:T(8,128)(2,1)} fusion(bf16[2048,8192]{1,0:T(8,128)(2,1)} %fusion.1, bf16[2048,128]{1,0:T(8,128)(2,1)S(1)} %all_gather.6), kind=kOutput, calls=%fused_computation.8 | convolution fusion | flops 4296015872 | bytes 36175872 | tf_op jit(solution)/shard_map/dot_general | solution.py:31
  357.0 618.7 %reduce-scatter.2.cloned.1.call-done = f32[16,128]{1,0:T(8,128)} async-done(((f32[2048,128]{1,0:T(8,128)}), f32[16,128]{1,0:T(8,128)}) %reduce-scatter.2.cloned.1.call-update) | async-done | bytes 8208 | tf_op jit(solution)/shard_map/reduce_scatter | solution.py:33
  975.6 0.9 fusion.6
  976.6 0.0 copy-done.2
  976.6 0.0 copy-done.3
  976.6 2.8 convolution_bitcast_fusion
  979.4 105.0 %all-reduce.3 = (bf16[768,768]{0,1:T(8,128)(2,1)}, bf16[768,128]{1,0:T(8,128)(2,1)}) all-reduce(f32[768,768]{0,1:T(8,128)} %convolution_bitcast_fusion, f32[768,128]{1,0:T(8,128)S(1)} %fusion.6), channel_id=1, replica_groups=mesh['dp'=1,'tp'=128] {'tp'}, use_global_device_ids=true, to_apply=%region_7.8 | all-reduce | flops 688128 | bytes 4128768 | tf_op jit(solution)/shard_map/psum | solution.py:38
  1084.4 2.4 copy.10
  (5 shorter events, 0.0 us)
Async XLA Ops:
  7.2 106.9 %copy-start = (bf16[8192,128]{1,0:T(8,128)(2,1)S(1)}, bf16[8192,128]{1,0:T(8,128)(2,1)}, u32[]{:S(2)}) copy-start(bf16[8192,128]{1,0:T(8,128)(2,1)} %param.9) | copy-start | bytes 6291460
  7.2 192.8 %copy-start.1 = (f32[8192]{0:T(1024)S(1)}, f32[8192]{0:T(1024)}, u32[]{:S(2)}) copy-start(f32[8192]{0:T(1024)} %param.10) | copy-start | bytes 98308
  7.2 968.4 %reduce-scatter.2.cloned.1.call-start = ((), (), s32[]{:S(2)}) async-start(), calls=%async_computation.1 | async-start | bytes 1056768 | tf_op jit(solution)/shard_map/reduce_scatter | solution.py:33
  323.6 653.0 %copy-start.2 = (bf16[768,128]{1,0:T(8,128)(2,1)S(1)}, bf16[768,128]{1,0:T(8,128)(2,1)}, u32[]{:S(2)}) copy-start(bf16[768,128]{1,0:T(8,128)(2,1)} %param.8) | copy-start | bytes 589828
  323.6 653.0 %copy-start.3 = (bf16[16,768]{1,0:T(8,128)(2,1)S(1)}, bf16[16,768]{1,0:T(8,128)(2,1)}, u32[]{:S(2)}) copy-start(bf16[16,768]{1,0:T(8,128)(2,1)} %param.6) | copy-start | bytes 73732
Sparse Core Ops, SparseCore 0:
  339.8 635.7 reduce-scatter.1
where the time goes:
time: 1100 us; the launch traced here: 1090 us
  waiting for transfers between devices  619 us (56%)
  blocking collectives  335 us (30%)
  matrix products  62.8 us (6%)
  other arithmetic  59.3 us (5%)
  between operations  15.9 us (1%)
    reduce_scatter x1, waiting for transfers between devices, local_step(): lax.psum_scatter(emb_part, 'tp', scatter_dimension=0, tiled=True)  619 us
    psum x1, blocking collectives, local_step(): grad_first, grad_second = lax.psum((first_part, second_part), 'tp')  105 us
    unnamed x1, blocking collectives  68.7 us
    psum x1, blocking collectives, local_step(): row_stats = lax.psum(jnp.stack([local_sum * rescale, local_target]), 'tp')  64.3 us
    pmax x1, blocking collectives, local_step(): row_max = lax.pmax(local_max, 'tp')  62.1 us
    all_gather x1, blocking collectives, local_step(): emb_all = lax.all_gather(query_emb, 'tp', axis=0, tiled=True)  34.5 us
    convert_element_type x1, other arithmetic, local_step(): (jnp.where(label_hit, soft_prob - 1.0, soft_prob) / total_rows).astype(jn...  33.7 us
    reduce_sum x1, other arithmetic, local_step(): local_sum = jnp.sum(exp_local, axis=1)  25 us
  transfers between devices with their start and end apart: 1, of which 1 were waited for; matrix products, arithmetic and copies ran while one was open for 2% of the time, Pallas kernels for 0%

commit v1 on v0

v1 whole, which is shorter than its diff:
```python
import jax
import jax.numpy as jnp
from jax import lax
from jax.experimental import pallas as pl
from jax.experimental.pallas import tpu as pltpu
from jax.sharding import PartitionSpec as P

MESH = pl.DeviceIdType.MESH
DMA = pltpu.SemaphoreType.DMA


def peer(index):
    return {"tp": index}


def entry_barrier(me, n):
    barrier = pltpu.get_barrier_semaphore()

    @pl.loop(1, n)
    def _(k):
        pl.semaphore_signal(barrier, inc=1, device_id=peer(lax.rem(me + k, n)), device_id_type=MESH)

    pl.semaphore_wait(barrier, n - 1)


def drain(ref, sem):
    pltpu.make_async_copy(ref, ref, sem).wait()


def gather_kernel(n, emb_ref, lab_ref, q_ref, emb_all, lab_all, q_all, sems):
    me = lax.axis_index("tp")
    core, chip, chips = lax.rem(me, 2), me // 2, n // 2
    entry_barrier(me, n)
    emb_all[pl.ds(me, 1)] = emb_ref[...][None]
    lab_all[pl.ds(me, 1)] = lab_ref[...]
    q_all[core, pl.ds(chip, 1)] = q_ref[...][None]

    @pl.loop(1, n)
    def _(k):
        to = peer(lax.rem(me + k, n))
        pltpu.make_async_remote_copy(emb_ref, emb_all.at[me], sems.at[0], sems.at[1], device_id=to, device_id_type=MESH).start()
        pltpu.make_async_remote_copy(lab_ref.at[0], lab_all.at[me], sems.at[2], sems.at[3], device_id=to, device_id_type=MESH).start()

    @pl.loop(1, chips)
    def _(k):
        to = peer(lax.rem(chip + k, chips) * 2 + core)
        pltpu.make_async_remote_copy(q_ref, q_all.at[core, chip], sems.at[4], sems.at[5], device_id=to, device_id_type=MESH).start()

    for ref, s in ((emb_all.at[pl.ds(0, n - 1)], 0), (lab_all.at[pl.ds(0, n - 1)], 2), (q_all.at[0, pl.ds(0, chips - 1)], 4)):
        drain(ref, sems.at[s])
        drain(ref, sems.at[s + 1])
    swap = pltpu.make_async_remote_copy(q_all.at[core], q_all.at[core], sems.at[6], sems.at[7], device_id=peer(chip * 2 + 1 - core), device_id_type=MESH)
    swap.start()
    swap.wait_send()
    drain(q_all.at[0], sems.at[7])


def stats_kernel(n, part_ref, out_all, got, mine, sems):
    me = lax.axis_index("tp")
    entry_barrier(me, n)

    @pl.loop(1, n)
    def _(k):
        p = lax.rem(me + k, n)
        pltpu.make_async_remote_copy(part_ref.at[p], got.at[me], sems.at[0], sems.at[1], device_id=peer(p), device_id_type=MESH).start()

    got[pl.ds(me, 1)] = part_ref[pl.ds(me, 1)]
    w = got.at[pl.ds(0, n - 1)]
    drain(w, sems.at[0])
    drain(w, sems.at[1])
    top = jnp.max(got[:, 0:1, :], axis=0, keepdims=True)
    total = jnp.sum(got[:, 1:2, :] * jnp.exp(got[:, 0:1, :] - top), axis=0, keepdims=True)
    target = jnp.sum(got[:, 2:3, :], axis=0, keepdims=True)
    mine[:, 0:1, :] = top
    mine[:, 1:2, :] = total
    mine[:, 2:3, :] = target
    mine[:, 3:8, :] = jnp.zeros((1, 5, 128), jnp.float32)
    out_all[pl.ds(me, 1)] = mine[...]

    @pl.loop(1, n)
    def _(k):
        p = lax.rem(me + k, n)
        pltpu.make_async_remote_copy(mine.at[0], out_all.at[me], sems.at[2], sems.at[3], device_id=peer(p), device_id_type=MESH).start()

    w = out_all.at[pl.ds(0, n - 1)]
    drain(w, sems.at[2])
    drain(w, sems.at[3])


def grad_kernel(n, part_ref, out_all, got, mine, sems):
    me = lax.axis_index("tp")
    entry_barrier(me, n)

    @pl.loop(1, n)
    def _(k):
        p = lax.rem(me + k, n)
        pltpu.make_async_remote_copy(part_ref.at[p], got.at[me], sems.at[0], sems.at[1], device_id=peer(p), device_id_type=MESH).start()

    got[pl.ds(me, 1)] = part_ref[pl.ds(me, 1)]
    w = got.at[pl.ds(0, n - 1)]
    drain(w, sems.at[0])
    drain(w, sems.at[1])
    mine[...] = jnp.sum(got[...], axis=0).astype(jnp.bfloat16)
    out_all[pl.ds(me, 1)] = mine[...][None]

    @pl.loop(1, n)
    def _(k):
        p = lax.rem(me + k, n)
        pltpu.make_async_remote_copy(mine, out_all.at[me], sems.at[2], sems.at[3], device_id=peer(p), device_id_type=MESH).start()

    w = out_all.at[pl.ds(0, n - 1)]
    drain(w, sems.at[2])
    drain(w, sems.at[3])


VMEM = pl.BlockSpec(memory_space=pltpu.VMEM)


def comm_call(kernel, n, name, collective_id, outs, scratch, sems, ins):
    import functools

    return pl.pallas_call(
        functools.partial(kernel, n),
        name=name,
        out_shape=outs,
        in_specs=[VMEM] * len(ins),
        out_specs=jax.tree.map(lambda _: VMEM, outs),
        scratch_shapes=scratch + [DMA((sems,))],
        compiler_params=pltpu.CompilerParams(collective_id=collective_id, has_side_effects=True, vmem_limit_bytes=40 << 20),
    )(*ins)


def solution(mesh):
    n = mesh.shape["tp"]
    f32, bf16 = jnp.float32, jnp.bfloat16

    def local_step(queries, w_first, w_second, catalogue, log_q, labels):
        rows = queries.shape[0]
        items_local = catalogue.shape[0]
        shard_index = lax.axis_index("tp")
        pre_act = jnp.dot(queries, w_first, preferred_element_type=f32)
        hidden = jnp.maximum(pre_act, 0.0).astype(bf16)
        query_emb = jnp.dot(hidden, w_second, preferred_element_type=f32).astype(bf16)
        lab_pad = jnp.pad(labels, (0, 128 - rows)).reshape(1, 1, 128)
        emb_all, lab_all, q_all = comm_call(
            gather_kernel, n, "gather", 0,
            (jax.ShapeDtypeStruct((n, rows, 128), bf16), jax.ShapeDtypeStruct((n, 1, 128), jnp.int32), jax.ShapeDtypeStruct((2, n // 2, rows, queries.shape[1]), bf16)),
            [], 8, (query_emb, lab_pad, queries))
        emb_all = emb_all.reshape(n * rows, 128)
        q_all = q_all.transpose(1, 0, 2, 3).reshape(n * rows, -1)
        labels_all = lab_all[:, 0, :rows].reshape(n * rows)
        total_rows = n * rows
        logits = lax.dot_general(emb_all, catalogue, (((1,), (1,)), ((), ())), preferred_element_type=f32) - log_q[None, :]
        local_max = jnp.max(logits, axis=1)
        local_ids = labels_all - shard_index * items_local
        label_hit = lax.broadcasted_iota(jnp.int32, (1, items_local), 1) == local_ids[:, None]
        local_target = jnp.sum(jnp.where(label_hit, logits, 0.0), axis=1)
        exp_local = jnp.exp(logits - local_max[:, None])
        local_sum = jnp.sum(exp_local, axis=1)
        stats = jnp.stack([local_max, local_sum, local_target]).reshape(3, n, rows).transpose(1, 0, 2)
        stats = jnp.pad(stats, ((0, 0), (0, 5), (0, 128 - rows)))
        stats_all = comm_call(stats_kernel, n, "stats", 1, jax.ShapeDtypeStruct((n, 8, 128), f32),
                              [pltpu.VMEM((n, 8, 128), f32), pltpu.VMEM((1, 8, 128), f32)], 4, (stats,))
        row_max, sum_exp, target = (stats_all[:, i, :rows].reshape(total_rows) for i in range(3))
        mean_loss = jnp.mean(row_max + jnp.log(sum_exp) - target).reshape(1)
        soft_prob = exp_local * (jnp.exp(local_max - row_max) / sum_exp)[:, None]
        grad_logits = (jnp.where(label_hit, soft_prob - 1.0, soft_prob) / total_rows).astype(bf16)
        grad_items = lax.dot_general(grad_logits, emb_all, (((0,), (0,)), ((), ())), preferred_element_type=f32).astype(bf16)
        emb_part = jnp.dot(grad_logits, catalogue, preferred_element_type=f32)
        grad_emb = comm_call(grad_kernel, n, "grads", 2, jax.ShapeDtypeStruct((n, rows, 128), bf16),
                             [pltpu.VMEM((n, rows, 128), f32), pltpu.VMEM((rows, 128), bf16)], 4, (emb_part.reshape(n, rows, 128),))
        grad_emb = grad_emb.reshape(total_rows, 128)
        pre_all = jnp.dot(q_all, w_first, preferred_element_type=f32)
        hid_all = jnp.maximum(pre_all, 0.0).astype(bf16)
        grad_second = lax.dot_general(hid_all, grad_emb, (((0,), (0,)), ((), ())), preferred_element_type=f32).astype(bf16)
        grad_hidden = lax.dot_general(grad_emb, w_second, (((1,), (1,)), ((), ())), preferred_element_type=f32)
        grad_pre = jnp.where(pre_all > 0.0, grad_hidden, 0.0).astype(bf16)
        grad_first = lax.dot_general(q_all, grad_pre, (((0,), (0,)), ((), ())), preferred_element_type=f32).astype(bf16)
        return mean_loss, grad_items, grad_first, grad_second

    row_spec = P(("dp", "tp"), None)
    return jax.shard_map(local_step, mesh=mesh, in_specs=(row_spec, P(None, None), P(None, None), P("tp", None), P("tp"), P(("dp", "tp"))), out_specs=(P("dp"), row_spec, P("dp", None), P("dp", None)), check_vma=False)
```

time: 1100 us -> 245 us (0.22)
  waiting for transfers between devices: 619 us -> 0 us
  blocking collectives: 335 us -> 0 us
  Pallas kernels: 0 us -> 101 us
  between operations: 15.9 us -> 2.55 us
  matrix products: 62.8 us -> 75.8 us
    reduce_scatter x1 -> x0, waiting for transfers between devices: 619 us -> none  [local_step(): lax.psum_scatter(emb_part, 'tp', scatter_dimension=0, tiled=True)]
    psum x2 -> x0, blocking collectives: 169 us -> none  [the longest x1 105 us: local_step(): grad_first, grad_second = lax.psum((first_part, second_part), 'tp')]
    pallas_call x0 -> x3, Pallas kernels: none -> 101 us  [comm_call(): pl.pallas_call(functools.partial(kernel, n), name=name, out_shape=outs, i...]
    unnamed x1 -> x0, blocking collectives: 68.7 us -> none
    pmax x1 -> x0, blocking collectives: 62.1 us -> none  [local_step(): row_max = lax.pmax(local_max, 'tp')]
    all_gather x1 -> x0, blocking collectives: 34.5 us -> none  [local_step(): emb_all = lax.all_gather(query_emb, 'tp', axis=0, tiled=True)]
    dot_general x5, matrix products: 22.4 us -> 35.2 us  [the longest x1 14.7 us: local_step(): emb_part = jnp.dot(grad_logits, catalogue, preferred_element_type=f32)]
  transfers between devices with their start and end apart: 1 -> 0, of which waited for: 1 -> 0; matrix products, arithmetic and copies ran while one was open for 2% -> 0% of each run, Pallas kernels for 0% -> 0%
where the time goes in v1:
time: 245 us
  Pallas kernels  101 us (41%)
  matrix products  75.8 us (31%)
  other arithmetic  60.2 us (25%)
  local copies, waits for them, and re-layouts  5.72 us (2%)
  between operations  2.55 us (1%)
    pallas_call x3, Pallas kernels, comm_call(): pl.pallas_call(functools.partial(kernel, n), name=name, out_shape=outs, i...  101 us
    convert_element_type x1, other arithmetic, local_step(): (jnp.where(label_hit, soft_prob - 1.0, soft_prob) / total_rows).astype(bf16)  33.7 us
    reduce_sum x1, other arithmetic, local_step(): local_sum = jnp.sum(exp_local, axis=1)  25 us
    dot_general x1, matrix products, local_step(): lax.dot_general(emb_all, catalogue, (((1,), (1,)), ((), ())), preferred_e...  23.8 us
    dot_general x1, matrix products, local_step(): lax.dot_general(grad_logits, emb_all, (((0,), (0,)), ((), ())), preferred...  16.8 us
    dot_general x1, matrix products, local_step(): emb_part = jnp.dot(grad_logits, catalogue, preferred_element_type=f32)  14.7 us
    dot_general x1, matrix products, local_step(): lax.dot_general(q_all, grad_pre, (((0,), (0,)), ((), ())), preferred_elem...  9.67 us

profile of v1, /device:TPU:1, one launch (start us, length us, event | category | flops | bytes accessed | tf_op | source)
XLA Modules:
  0.0 245.1 jit_solution(1082622952405396936)
XLA Ops:
  0.6 0.0 copy-start
  0.6 1.8 fusion.10.emb_ref
  2.5 0.7 pad_bitcast_fusion.lab_ref
  3.2 0.0 copy-start.3
  3.2 0.7 copy-done.3
  3.9 44.1 %gather.1 = (bf16[128,16,128]{2,1,0:T(8,128)(2,1)S(1)}, s32[128,1,128]{2,1,0:T(1,128)S(1)}, bf16[2,64,16,768]{3,2,1,0:T(8,128)(2,1)S(1)}) custom-call(bf16[16,128]{1,0:T(8,128)(2,1)S(1)} %fusion.10.emb_ref, s32[1,1,128]{2,1,0:T(1,128)S(1)} %pad_bitcast_fusion.lab_ref, bf16[16,768]{1,0:T(8,128)(2,1)S(1)} %copy-done.3), custom_call_target="tpu_custom_call" | custom-call | tf_op jit(solution)/shard_map/gather/pallas_call | solution.py:122
  48.0 0.0 copy-start.1
  48.1 1.6 copy-done.1
  49.7 0.0 copy-done
  49.7 0.0 copy-start.5
  49.7 23.8 %subtract_reduce_fusion = (f32[2048]{0:T(1024)S(1)}, f32[2048,8192]{1,0:T(8,128)}) fusion(f32[8192]{0:T(1024)} %param.10, bf16[2048,128]{1,0:T(8,128)(2,1)S(1)} %bitcast.32, bf16[8192,128]{1,0:T(8,128)(2,1)S(1)} %copy-done), kind=kOutput, calls=%fused_computation.7 | convolution fusion | flops 4328519680 | bytes 69771264 | tf_op jit(solution)/shard_map/dot_general | solution.py:153
  73.5 0.2 subtract_reduce_fusion.2
  73.7 0.1 sub.50
  73.8 0.0 copy-done.5
  73.8 25.0 %fusion.2 = (f32[2048]{0:T(1024)S(1)}, f32[2048]{0:T(1024)S(1)}) fusion(f32[2048,8192]{1,0:T(8,128)} %get-tuple-element.16, f32[2048]{0:T(1024)S(1)} %get-tuple-element.15, f32[8192]{0:T(1024)S(1)} %copy-done.5, s32[2048]{0:T(1024)S(1)} %sub.50), kind=kLoop, calls=%fused_computation.6 | loop fusion | flops 100659200 | bytes 67174400 | tf_op jit(solution)/shard_map/reduce_sum | solution.py:159
  98.8 0.1 stack.14
  98.8 0.1 stack.13
  98.9 0.1 stack.12
  99.0 0.2 maximum_bitcast_fusion
  99.3 27.5 %stats.1 = f32[128,8,128]{2,1,0:T(8,128)S(1)} custom-call(f32[128,8,128]{2,1,0:T(8,128)S(1)} %pad.9.part_ref), custom_call_target="tpu_custom_call" | custom-call | tf_op jit(solution)/shard_map/stats/pallas_call | solution.py:122
  126.9 1.1 slice_reduce_fusion.1
  128.6 0.1 reshape_squeeze.9
  128.7 0.1 reshape_squeeze.8
  128.8 33.7 %fusion.1 = bf16[2048,8192]{1,0:T(8,128)(2,1)} fusion(f32[2048,8192]{1,0:T(8,128)} %get-tuple-element.16, f32[2048]{0:T(1024)S(1)} %exponential_divide_fusion, s32[2048]{0:T(1024)S(1)} %sub.50, f32[2048]{0:T(1024)S(1)} %get-tuple-element.15, f32[8192]{0:T(1024)S(1)} %copy-done.5), kind=kLoop, calls=%fused_computation.2 | loop fusion | flops 134217728 | bytes 100720640 | tf_op jit(solution)/shard_map/convert_element_type | solution.py:167
  162.5 0.0 copy-start.2
  162.5 16.8 %convolution_convert_fusion = bf16[8192,128]{1,0:T(8,128)(2,1)} fusion(bf16[2048,8192]{1,0:T(8,128)(2,1)} %fusion.1, bf16[2048,128]{1,0:T(8,128)(2,1)S(1)} %bitcast.33), kind=kOutput, calls=%fused_computation.8 | convolution fusion | flops 4296015872 | bytes 36175872 | tf_op jit(solution)/shard_map/dot_general | solution.py:168
  179.2 0.0 copy-start.6
  179.2 0.0 copy-done.2
  179.2 0.5 copy.22
  179.7 0.0 copy-start.4
  179.7 1.7 copy-done.4
  181.4 0.0 copy-done.6
  181.4 4.5 %fusion.15 = f32[2048,768]{1,0:T(8,128)} fusion(bf16[2048,768]{1,0:T(8,128)(2,1)S(1)} %bitcast.34, bf16[768,768]{1,0:T(8,128)(2,1)S(1)} %copy-done.6), kind=kOutput, calls=%fused_computation.31 | convolution fusion | flops 2415919104 | bytes 10616832 | tf_op jit(solution)/shard_map/dot_general | solution.py:173
  185.9 0.0 copy-start.7
  185.9 14.7 %fusion.16 = f32[2048,128]{1,0:T(8,128)S(1)} fusion(bf16[2048,8192]{1,0:T(8,128)(2,1)} %fusion.1, bf16[8192,128]{1,0:T(8,128)(2,1)S(1)} %copy-done), kind=kOutput, calls=%fused_computation.32 | convolution fusion | flops 4294967296 | bytes 36700160 | tf_op jit(solution)/shard_map/dot_general | solution.py:169
  200.6 29.2 %grads.1 = bf16[128,16,128]{2,1,0:T(8,128)(2,1)S(1)} custom-call(f32[128,16,128]{2,1,0:T(8,128)S(1)} %bitcast.31), custom_call_target="tpu_custom_call" | custom-call | tf_op jit(solution)/shard_map/grads/pallas_call | solution.py:122
  229.8 0.0 copy-done.7
  229.8 9.7 %fusion.6 = bf16[768,768]{1,0:T(8,128)(2,1)} fusion(bf16[2048,768]{1,0:T(8,128)(2,1)} %bitcast.35, f32[2048,768]{1,0:T(8,128)} %fusion.15, bf16[2048,128]{1,0:T(8,128)(2,1)S(1)} %bitcast.29, bf16[768,128]{1,0:T(8,128)(2,1)S(1)} %copy-done.7), kind=kOutput, calls=%fused_computation.14 | convolution fusion | flops 2823880704 | bytes 11337728 | tf_op jit(solution)/shard_map/dot_general | solution.py:178
  239.5 4.5 %fusion.7 = bf16[768,128]{1,0:T(8,128)(2,1)} fusion(bf16[2048,128]{1,0:T(8,128)(2,1)S(1)} %bitcast.30, f32[2048,768]{1,0:T(8,128)} %fusion.15), kind=kOutput, calls=%fused_computation.15 | convolution fusion | flops 405897216 | bytes 7012352 | tf_op jit(solution)/shard_map/dot_general | solution.py:175
  (2 shorter events, 0.1 us)
Async XLA Ops:
  0.6 49.0 %copy-start = (bf16[8192,128]{1,0:T(8,128)(2,1)S(1)}, bf16[8192,128]{1,0:T(8,128)(2,1)}, u32[]{:S(2)}) copy-start(bf16[8192,128]{1,0:T(8,128)(2,1)} %param.9) | copy-start | bytes 6291460
  3.2 0.7 copy-start.3
  48.0 1.6 copy-start.1
  49.7 24.1 %copy-start.5 = (f32[8192]{0:T(1024)S(1)}, f32[8192]{0:T(1024)}, u32[]{:S(2)}) copy-start(f32[8192]{0:T(1024)} %param.10) | copy-start | bytes 98308
  162.5 16.8 %copy-start.2 = (bf16[2,64,16,768]{3,2,1,0:T(8,128)(2,1)S(1)}, bf16[2,64,16,768]{3,2,1,0:T(8,128)(2,1)}, u32[]{:S(2)}) copy-start(bf16[2,64,16,768]{3,2,1,0:T(8,128)(2,1)} %copy-done.1) | copy-start | bytes 9437188
  179.2 2.2 copy-start.6
  179.7 1.7 copy-start.4
  185.9 43.9 %copy-start.7 = (bf16[768,128]{1,0:T(8,128)(2,1)S(1)}, bf16[768,128]{1,0:T(8,128)(2,1)}, u32[]{:S(2)}) copy-start(bf16[768,128]{1,0:T(8,128)(2,1)} %param.8) | copy-start | bytes 589828

commit v2 on v0

v2 whole, which is shorter than its diff:
```python
import functools
import math
import jax
import jax.numpy as jnp
from jax import lax
from jax.experimental import pallas as pl
from jax.experimental.pallas import tpu as pltpu
from jax.sharding import PartitionSpec as P

MESH = pl.DeviceIdType.MESH
DMA = pltpu.SemaphoreType.DMA
F32, BF16 = jnp.float32, jnp.bfloat16
LOG2E = 1.4426950408889634
BLOCKS = 8
QB = 256
SUB = 512
UNROLL = 4


def peer(index):
    return {"tp": index}


def drain(ref, sem):
    pltpu.make_async_copy(ref, ref, sem).wait()


def slot_of(d, n):
    core, chip = d % 2, d // 2
    if n == 128:
        x, y, z = chip % 4, (chip // 4) % 4, chip // 16
        return ((x + y + z) % 4) * 2 + core, z * 4 + y
    return (chip % 4) * 2 + core, chip // 4


def device_of(k, j, n):
    if n == 128:
        z, y = j // 4, j % 4
        x = (k // 2 + 8 - y - z) % 4
        return ((z * 4 + y) * 4 + x) * 2 + k % 2
    return (j * 4 + k // 2) * 2 + k % 2


def kernel(n, rows, items,
           q_ref, w1_hbm, w2_hbm, e_hbm, lq_ref, lab_ref,
           loss_ref, de_hbm, dw1_ref, dw2_ref,
           w1, w2, e, et, lqb, ids, x_mine, lab_mine, x_all, lab_all, q_all, xbt, zs,
           st_send, st_got, st_mine, st_all, de_acc, de_out, dxt, dx_part, dx_got, dx_mine, dx_all,
           t_acc, t_mine, t_all, pre, acc1, acc2,
           load_sem, out_sem, x_sem, lab_sem, q_sem, swap_sem, st_sem, stb_send, stb_recv, dx_sem, dxb_send, dxb_recv, t_sem):
    me = lax.axis_index("tp")
    ob = n // BLOCKS
    half = ob // 2
    my_k, my_j = slot_of(me, n)
    my_slot = my_k * ob + my_j
    core, chip, chips = me % 2, me // 2, n // 2
    my_row = core * chips + (my_k // 2) * ob + my_j

    loads = [pltpu.make_async_copy(a, b, load_sem.at[i]) for i, (a, b) in enumerate(((w1_hbm, w1), (w2_hbm, w2), (e_hbm, e)))]
    for c in loads:
        c.start()
    barrier = pltpu.get_barrier_semaphore()

    @pl.loop(1, n)
    def _(k):
        pl.semaphore_signal(barrier, inc=1, device_id=peer(lax.rem(me + k, n)), device_id_type=MESH)

    loads[0].wait()
    loads[1].wait()
    hid = jnp.maximum(jnp.dot(q_ref[...], w1[...], preferred_element_type=F32), 0.0).astype(BF16)
    x_mine[...] = jnp.dot(hid, w2[...], preferred_element_type=F32).astype(BF16)
    lanes = lax.broadcasted_iota(jnp.int32, (1, 128), 1)
    wide = jnp.concatenate([lab_ref[...]] * (128 // rows), axis=1) if rows < 128 else lab_ref[...]
    lab_mine[...] = jnp.where(lanes // rows == my_j % half, wide, 0)
    x_all[pl.ds(my_slot, 1)] = x_mine[...][None]
    lab_all[pl.ds(my_slot, 1)] = lab_mine[...][None]
    q_all[pl.ds(my_row, 1)] = q_ref[...][None]
    pl.semaphore_wait(barrier, n - 1)

    @pl.loop(1, n)
    def _(k):
        to = peer(lax.rem(me + k, n))
        pltpu.make_async_remote_copy(x_mine, x_all.at[my_slot], x_sem.at[0], x_sem.at[1], device_id=to, device_id_type=MESH).start()
        pltpu.make_async_remote_copy(lab_mine, lab_all.at[my_slot], lab_sem.at[0], lab_sem.at[1], device_id=to, device_id_type=MESH).start()

    loads[2].wait()

    @pl.loop(0, items // 128)
    def _(i):
        r = pl.multiple_of(i * 128, 128)
        lqb[pl.ds(r, 128), :] = jnp.broadcast_to(lq_ref[pl.ds(i, 1), :], (128, 128)).T
        et[:, pl.ds(r, 128)] = e[pl.ds(r, 128), :].T
        de_acc[pl.ds(r, 128), :] = jnp.zeros((128, 128), F32)

    ids[...] = lax.broadcasted_iota(jnp.int32, (SUB, 128), 0)
    t_acc[...] = jnp.zeros_like(t_acc)
    acc1[...] = jnp.zeros_like(acc1)
    acc2[...] = jnp.zeros_like(acc2)
    drain(x_all.at[pl.ds(0, n - 1)], x_sem.at[1])
    drain(lab_all.at[pl.ds(0, n - 1)], lab_sem.at[1])

    def combine_stats(k):
        @pl.when(jnp.logical_and(my_k == k, my_j % half == 0))
        def _():
            drain(st_got.at[pl.ds(0, n - 1)], st_sem.at[1])
            top = jnp.max(st_got[:, 0:1, :], axis=0)
            total = jnp.sum(st_got[:, 1:2, :] * jnp.exp(st_got[:, 0:1, :] - top[None]), axis=0)
            st_mine[...] = jnp.concatenate([top, jnp.log(total)], axis=0)
            st_all[pl.ds(k * 2 + my_j // half, 1)] = st_mine[...][None]

            @pl.loop(1, n)
            def _(i):
                pltpu.make_async_remote_copy(st_mine, st_all.at[k * 2 + my_j // half], stb_send, stb_recv.at[k * 2 + my_j // half],
                                             device_id=peer(lax.rem(me + i, n)), device_id_type=MESH).start()

    def combine_rows(k):
        @pl.when(my_k == k)
        def _():
            drain(dx_got.at[pl.ds(0, n - 1)], dx_sem.at[1])
            dx_mine[...] = jnp.sum(dx_got[...], axis=0).astype(BF16)
            dx_all[pl.ds(my_slot, 1)] = dx_mine[...][None]

            @pl.loop(1, n)
            def _(i):
                pltpu.make_async_remote_copy(dx_mine, dx_all.at[my_slot], dxb_send, dxb_recv.at[k],
                                             device_id=peer(lax.rem(me + i, n)), device_id_type=MESH).start()

    def logits(r):
        lq = lqb[pl.ds(r, SUB), :]
        z = jnp.dot(e[pl.ds(r, SUB), :], xbt[...], preferred_element_type=F32)
        return z - jnp.concatenate([lq, lq], axis=1)

    @pl.loop(0, BLOCKS)
    def _(k):
        xbt[...] = x_all[pl.ds(k * ob, ob)].reshape(QB, 128).T

        def step(i, carry):
            m, s = carry
            for u in range(UNROLL):
                z = logits(pl.multiple_of((i * UNROLL + u) * SUB, SUB)).reshape(SUB // 8, 8, QB)
                m_new = jnp.maximum(m, jnp.max(z, axis=0))
                s = s * jnp.exp2((m - m_new) * LOG2E) + jnp.sum(jnp.exp2((z - m_new[None]) * LOG2E), axis=0)
                m = m_new
            return m, s

        m, s = lax.fori_loop(0, items // (SUB * UNROLL), step, (jnp.full((8, QB), -3.0e38, F32), jnp.zeros((8, QB), F32)))
        top = jnp.max(m, axis=0, keepdims=True)
        total = jnp.sum(s * jnp.exp2((m - top) * LOG2E), axis=0, keepdims=True)
        for t in range(2):
            st_send[pl.ds(k * 2 + t, 1)] = jnp.concatenate([top[:, t * 128:(t + 1) * 128], total[:, t * 128:(t + 1) * 128]], axis=0)[None]
        for t in range(2):
            to = device_of(k, t * half, n)

            @pl.when(to != me)
            def _():
                pltpu.make_async_remote_copy(st_send.at[k * 2 + t], st_got.at[me], st_sem.at[0], st_sem.at[1], device_id=peer(to), device_id_type=MESH).start()

            @pl.when(to == me)
            def _():
                st_got[pl.ds(me, 1)] = st_send[pl.ds(k * 2 + t, 1)]

        combine_stats(k - 4)

    per_step = -(-(chips - 1) // (BLOCKS - 1))

    @pl.loop(0, BLOCKS)
    def _(k):
        @pl.loop(0, per_step)
        def _(i):
            c = k * per_step + i + 1

            @pl.when(c < chips)
            def _():
                pltpu.make_async_remote_copy(q_ref, q_all.at[my_row], q_sem.at[0], q_sem.at[1],
                                             device_id=peer(lax.rem(chip + c, chips) * 2 + core), device_id_type=MESH).start()

        for t in range(2):
            @pl.when(device_of(k, t * half, n) != me)
            def _():
                drain(st_all.at[0], stb_recv.at[k * 2 + t])

        xb = x_all[pl.ds(k * ob, ob)].reshape(QB, 128)
        xbt[...] = xb.T
        top = jnp.concatenate([st_all[k * 2, 0:1, :], st_all[k * 2 + 1, 0:1, :]], axis=1)
        shift = jnp.concatenate([st_all[k * 2, 1:2, :], st_all[k * 2 + 1, 1:2, :]], axis=1) * LOG2E + math.log2(n * rows)
        lab = jnp.concatenate([jnp.sum(lab_all[pl.ds(k * ob + t * half, half)], axis=0) for t in range(2)], axis=1) - me * items
        dxt[...] = jnp.zeros_like(dxt)

        @pl.loop(0, items // (SUB * UNROLL))
        def _(i):
            dx = dxt[...]
            tsum = t_acc[...]
            for u in range(UNROLL):
                r = pl.multiple_of((i * UNROLL + u) * SUB, SUB)
                z = logits(r)
                idv = ids[...]
                hit = jnp.concatenate([idv, idv], axis=1) == lab - r
                g = jnp.exp2((z - top) * LOG2E - shift) - jnp.where(hit, 1.0 / (n * rows), 0.0)
                tsum = tsum + jnp.sum(jnp.where(hit, z, 0.0).reshape(SUB // 8, 8, QB), axis=0)
                gb = g.astype(BF16)
                de_acc[pl.ds(r, SUB), :] += jnp.dot(gb, xb, preferred_element_type=F32)
                dx = dx + jnp.dot(et[:, pl.ds(r, SUB)], gb, preferred_element_type=F32)
            dxt[...] = dx
            t_acc[...] = tsum

        dx_part[pl.ds(k * ob, ob)] = dxt[...].T.reshape(ob, rows, 128)

        @pl.loop(0, ob)
        def _(j):
            to = device_of(k, j, n)

            @pl.when(to != me)
            def _():
                pltpu.make_async_remote_copy(dx_part.at[k * ob + j], dx_got.at[me], dx_sem.at[0], dx_sem.at[1], device_id=peer(to), device_id_type=MESH).start()

            @pl.when(to == me)
            def _():
                dx_got[pl.ds(me, 1)] = dx_part[pl.ds(k * ob + j, 1)]

        @pl.when(k < 4)
        def _():
            combine_stats(k + 4)

        combine_rows(k - 2)

    t_mine[...] = jnp.sum(t_acc[:, 0:128] + t_acc[:, 128:256], axis=0, keepdims=True)
    t_all[pl.ds(me, 1)] = t_mine[...][None]

    @pl.loop(1, n)
    def _(i):
        pltpu.make_async_remote_copy(t_mine, t_all.at[me], t_sem.at[0], t_sem.at[1], device_id=peer(lax.rem(me + i, n)), device_id_type=MESH).start()

    drain(q_all.at[pl.ds(0, chips - 1)], q_sem.at[1])
    swap = pltpu.make_async_remote_copy(q_all.at[pl.ds(core * chips, chips)], q_all.at[pl.ds(core * chips, chips)], swap_sem.at[0], swap_sem.at[1], device_id=peer(chip * 2 + 1 - core), device_id_type=MESH)
    swap.start()

    @pl.loop(0, items // SUB)
    def _(i):
        r = pl.multiple_of(i * SUB, SUB)
        de_out[pl.ds(r, SUB), :] = de_acc[pl.ds(r, SUB), :].astype(BF16)

    out = pltpu.make_async_copy(de_out, de_hbm, out_sem)
    out.start()
    drain(q_all.at[pl.ds(0, chips)], swap_sem.at[1])

    def rows_of(k):
        return q_all[pl.ds((k % 2) * chips + (k // 2) * ob, ob)].reshape(QB, q_all.shape[-1])

    @pl.loop(0, BLOCKS)
    def _(k):
        pre[pl.ds(k, 1)] = jnp.dot(rows_of(k), w1[...], preferred_element_type=F32)[None]

    def tower(k):
        @pl.when(my_k == k)
        def _():
            if ob > 1:
                drain(dx_all.at[pl.ds(0, ob - 1)], dxb_recv.at[k])

        @pl.when(my_k != k)
        def _():
            drain(dx_all.at[pl.ds(0, ob)], dxb_recv.at[k])

        dx = dx_all[pl.ds(k * ob, ob)].reshape(QB, 128)
        a = pre[k]
        h = jnp.maximum(a, 0.0).astype(BF16)
        acc2[...] += lax.dot_general(h, dx, (((0,), (0,)), ((), ())), preferred_element_type=F32)
        dh = lax.dot_general(dx, w2[...], (((1,), (1,)), ((), ())), preferred_element_type=F32)
        da = jnp.where(a > 0.0, dh, 0.0).astype(BF16)
        acc1[...] += lax.dot_general(rows_of(k), da, (((0,), (0,)), ((), ())), preferred_element_type=F32)

    combine_rows(BLOCKS - 2)
    pl.loop(0, BLOCKS - 3)(tower)
    combine_rows(BLOCKS - 1)
    pl.loop(BLOCKS - 3, BLOCKS)(tower)
    dw1_ref[...] = acc1[...].astype(BF16)
    dw2_ref[...] = acc2[...].astype(BF16)

    drain(t_all.at[pl.ds(0, n - 1)], t_sem.at[1])
    lse = st_all[:, 0:1, :] + st_all[:, 1:2, :]
    total = jnp.sum(lse, axis=0) - jnp.sum(t_all[...], axis=0)
    loss_ref[0] = jnp.sum(total) / (n * rows)

    out.wait()
    swap.wait_send()
    drain(x_all.at[pl.ds(0, n - 1)], x_sem.at[0])
    drain(lab_all.at[pl.ds(0, n - 1)], lab_sem.at[0])
    drain(q_all.at[pl.ds(0, chips - 1)], q_sem.at[0])
    drain(t_all.at[pl.ds(0, n - 1)], t_sem.at[0])
    drain(dx_got.at[pl.ds(0, n - 1)], dx_sem.at[0])

    @pl.when(my_j % half == 0)
    def _():
        drain(st_got.at[pl.ds(0, n - 1)], stb_send)
        drain(st_got.at[pl.ds(0, 2 * BLOCKS - 1)], st_sem.at[0])

    @pl.when(my_j % half != 0)
    def _():
        drain(st_got.at[pl.ds(0, 2 * BLOCKS)], st_sem.at[0])

    drain(dx_all.at[pl.ds(0, n - 1)], dxb_send)


def solution(mesh):
    n = mesh.shape["tp"]

    def local_step(queries, w_first, w_second, catalogue, log_q, labels):
        rows, width = queries.shape
        items = catalogue.shape[0]
        hidden = w_first.shape[1]
        ob = n // BLOCKS
        V, ANY = pl.BlockSpec(memory_space=pltpu.VMEM), pl.BlockSpec(memory_space=pl.ANY)
        S = jax.ShapeDtypeStruct
        M = pltpu.VMEM
        i32 = jnp.int32
        loss, grad_items, grad_first, grad_second = pl.pallas_call(
            functools.partial(kernel, n, rows, items),
            name="two_tower",
            out_shape=(S((1,), F32), S((items, 128), BF16), S((width, hidden), BF16), S((hidden, 128), BF16)),
            in_specs=[V, ANY, ANY, ANY, V, V],
            out_specs=(pl.BlockSpec(memory_space=pltpu.SMEM), ANY, V, V),
            scratch_shapes=[
                M((width, hidden), BF16), M((hidden, 128), BF16), M((items, 128), BF16), M((128, items), BF16), M((items, 128), F32), M((SUB, 128), i32),
                M((rows, 128), BF16), M((1, 128), i32), M((n, rows, 128), BF16), M((n, 1, 128), i32), M((n, rows, width), BF16), M((128, QB), BF16), M((8, 128), F32),
                M((2 * BLOCKS, 2, 128), F32), M((n, 2, 128), F32), M((2, 128), F32), M((2 * BLOCKS, 2, 128), F32), M((items, 128), F32), M((items, 128), BF16), M((128, QB), F32),
                M((n, rows, 128), F32), M((n, rows, 128), F32), M((rows, 128), BF16), M((n, rows, 128), BF16),
                M((8, QB), F32), M((1, 128), F32), M((n, 1, 128), F32), M((BLOCKS, QB, hidden), F32), M((width, hidden), F32), M((hidden, 128), F32),
                DMA((3,)), DMA, DMA((2,)), DMA((2,)), DMA((2,)), DMA((2,)), DMA((2,)), DMA, DMA((2 * BLOCKS,)), DMA((2,)), DMA, DMA((BLOCKS,)), DMA((2,)),
            ],
            compiler_params=pltpu.CompilerParams(collective_id=0, has_side_effects=True, vmem_limit_bytes=60 << 20),
        )(queries, w_first, w_second, catalogue, log_q.reshape(items // 128, 128), labels.reshape(1, rows))
        return loss, grad_items, grad_first, grad_second

    row_spec = P(("dp", "tp"), None)
    return jax.shard_map(local_step, mesh=mesh, in_specs=(row_spec, P(None, None), P(None, None), P("tp", None), P("tp"), P(("dp", "tp"))), out_specs=(P("dp"), row_spec, P("dp", None), P("dp", None)), check_vma=False)
```

time: 1100 us -> 125 us (0.11)
  waiting for transfers between devices: 619 us -> 0 us
  blocking collectives: 335 us -> 0 us
  Pallas kernels: 0 us -> 118 us
  matrix products: 62.8 us -> 0 us
  other arithmetic: 59.3 us -> 0 us
  between operations: 15.9 us -> 2.4 us
    reduce_scatter x1 -> x0, waiting for transfers between devices: 619 us -> none  [local_step(): lax.psum_scatter(emb_part, 'tp', scatter_dimension=0, tiled=True)]
    psum x2 -> x0, blocking collectives: 169 us -> none  [the longest x1 105 us: local_step(): grad_first, grad_second = lax.psum((first_part, second_part), 'tp')]
    pallas_call x0 -> x1, Pallas kernels: none -> 118 us  [local_step(): pl.pallas_call(functools.partial(kernel, n, rows, items), name='two_tower...]
    unnamed x1 -> x0, blocking collectives: 68.7 us -> none
    dot_general x7 -> x0, matrix products: 62.8 us -> none  [the longest x1 23.8 us: local_step(): lax.dot_general(emb_all, catalogue, (((1,), (1,)), ((), ())), preferred_e...]
    pmax x1 -> x0, blocking collectives: 62.1 us -> none  [local_step(): row_max = lax.pmax(local_max, 'tp')]
    all_gather x1 -> x0, blocking collectives: 34.5 us -> none  [local_step(): emb_all = lax.all_gather(query_emb, 'tp', axis=0, tiled=True)]
    convert_element_type x1 -> x0, other arithmetic: 33.7 us -> none  [local_step(): (jnp.where(label_hit, soft_prob - 1.0, soft_prob) / total_rows).astype(jn...]
  transfers between devices with their start and end apart: 1 -> 0, of which waited for: 1 -> 0; matrix products, arithmetic and copies ran while one was open for 2% -> 0% of each run, Pallas kernels for 0% -> 0%
where the time goes in v2:
time: 125 us
  Pallas kernels  118 us (94%)
  local copies, waits for them, and re-layouts  4.94 us (4%)
  between operations  2.4 us (2%)
    pallas_call x1, Pallas kernels, local_step(): pl.pallas_call(functools.partial(kernel, n, rows, items), name='two_tower...  118 us
    unnamed x7, local copies, waits for them, and re-layouts  4.94 us

profile of v2, /device:TPU:1, one launch (start us, length us, event | category | flops | bytes accessed | tf_op | source)
XLA Modules:
  0.0 124.8 jit_solution(1836937027041141212)
XLA Ops:
  0.6 117.5 %two_tower.1 = (f32[1]{0:T(128)}, bf16[8192,128]{1,0:T(8,128)(2,1)}, bf16[768,768]{1,0:T(8,128)(2,1)}, bf16[768,128]{1,0:T(8,128)(2,1)}) custom-call(bf16[16,768]{1,0:T(8,128)(2,1)} %q_ref.1, bf16[768,768]{1,0:T(8,128)(2,1)} %w1_hbm.1, bf16[768,128]{1,0:T(8,128)(2,1)} %w2_hbm.1, bf16[8192,128]{1,0:T(8,128)(2,1)} %e_hbm.1, f32[64,128]{1,0:T(8,128)} %bitcast.2, ...), custom_call_target="tpu_custom_call" | custom-call | tf_op jit(solution)/shard_map/two_tower/pallas_call | solution.py:315
  118.8 0.0 copy-start
  118.8 3.1 %copy.15 = bf16[8192,128]{1,0:T(8,128)(2,1)} copy(bf16[8192,128]{1,0:T(8,128)(2,1)} %get-tuple-element.9) | data formatting | bytes 4194304
  121.9 0.0 copy-done
  121.9 0.0 copy-start.1
  121.9 1.0 copy.16
  122.9 0.1 copy-done.1
  123.0 0.7 copy.17
Async XLA Ops:
  118.8 3.2 %copy-start = (bf16[768,768]{1,0:T(8,128)(2,1)S(1)}, bf16[768,768]{1,0:T(8,128)(2,1)}, u32[]{:S(2)}) copy-start(bf16[768,768]{1,0:T(8,128)(2,1)} %get-tuple-element.10) | copy-start | bytes 3538948
  121.9 1.1 copy-start.1

commit v3 on v2

--- a/solution.py
+++ b/solution.py
@@ -12,9 +12,10 @@
 F32, BF16 = jnp.float32, jnp.bfloat16
 LOG2E = 1.4426950408889634
 BLOCKS = 8
+LOW = -3.0e38
 QB = 256
 SUB = 512
-UNROLL = 4
+UNROLL = 16
 
 
 def peer(index):
@@ -41,13 +42,28 @@
     return (j * 4 + k // 2) * 2 + k % 2
 
 
+def split3(v):
+    big = float(jnp.finfo(BF16).max)
+    a = jnp.clip(v, -big, big).astype(BF16).astype(F32)
+    b = (v - a).astype(BF16).astype(F32)
+    return [a, b, v - a - b]
+
+
+def stack_rows(values, height, width=128):
+    at = lax.broadcasted_iota(jnp.int32, (height, width), 0)
+    out = jnp.zeros((height, width), F32)
+    for i, v in enumerate(values):
+        out = jnp.where(at == i, v, out)
+    return out
+
+
 def kernel(n, rows, items,
            q_ref, w1_hbm, w2_hbm, e_hbm, lq_ref, lab_ref,
            loss_ref, de_hbm, dw1_ref, dw2_ref,
-           w1, w2, e, et, lqb, ids, x_mine, lab_mine, x_all, lab_all, q_all, xbt, zs,
+           w1, w2, e, et, ids, x_mine, lab_mine, x_all, lab_all, q_all, xa, xb, za, zb, ga, gb,
            st_send, st_got, st_mine, st_all, de_acc, de_out, dxt, dx_part, dx_got, dx_mine, dx_all,
            t_acc, t_mine, t_all, pre, acc1, acc2,
-           load_sem, out_sem, x_sem, lab_sem, q_sem, swap_sem, st_sem, stb_send, stb_recv, dx_sem, dxb_send, dxb_recv, t_sem):
+           load_sem, out_sem, x_sem, xs_sem, lab_sem, q_sem, swap_sem, st_sem, stb_send, stb_recv, dx_sem, dxb_send, dxb_recv, t_sem):
     me = lax.axis_index("tp")
     ob = n // BLOCKS
     half = ob // 2
@@ -56,7 +72,14 @@
     core, chip, chips = me % 2, me // 2, n // 2
     my_row = core * chips + (my_k // 2) * ob + my_j
 
-    loads = [pltpu.make_async_copy(a, b, load_sem.at[i]) for i, (a, b) in enumerate(((w1_hbm, w1), (w2_hbm, w2), (e_hbm, e)))]
+    def row0(k):
+        return (k % 2) * chips + (k // 2) * ob
+
+    def swap_cores(ref, sem):
+        part = ref.at[pl.ds(core * chips, chips)]
+        return pltpu.make_async_remote_copy(part, part, sem.at[0], sem.at[1], device_id=peer(chip * 2 + 1 - core), device_id_type=MESH)
+
+    loads = [pltpu.make_async_copy(a, b, load_sem.at[i]) for i, (a, b) in enumerate(((w1_hbm, w1), (w2_hbm, w2), (e_hbm, e.at[:, 0:128])))]
     for c in loads:
         c.start()
     barrier = pltpu.get_barrier_semaphore()
@@ -72,32 +95,41 @@
     lanes = lax.broadcasted_iota(jnp.int32, (1, 128), 1)
     wide = jnp.concatenate([lab_ref[...]] * (128 // rows), axis=1) if rows < 128 else lab_ref[...]
     lab_mine[...] = jnp.where(lanes // rows == my_j % half, wide, 0)
-    x_all[pl.ds(my_slot, 1)] = x_mine[...][None]
-    lab_all[pl.ds(my_slot, 1)] = lab_mine[...][None]
+    x_all[pl.ds(my_row, 1)] = x_mine[...][None]
+    lab_all[pl.ds(my_row, 1)] = lab_mine[...][None]
     q_all[pl.ds(my_row, 1)] = q_ref[...][None]
-    pl.semaphore_wait(barrier, n - 1)
-
-    @pl.loop(1, n)
-    def _(k):
-        to = peer(lax.rem(me + k, n))
-        pltpu.make_async_remote_copy(x_mine, x_all.at[my_slot], x_sem.at[0], x_sem.at[1], device_id=to, device_id_type=MESH).start()
-        pltpu.make_async_remote_copy(lab_mine, lab_all.at[my_slot], lab_sem.at[0], lab_sem.at[1], device_id=to, device_id_type=MESH).start()
-
     loads[2].wait()
 
     @pl.loop(0, items // 128)
     def _(i):
         r = pl.multiple_of(i * 128, 128)
-        lqb[pl.ds(r, 128), :] = jnp.broadcast_to(lq_ref[pl.ds(i, 1), :], (128, 128)).T
-        et[:, pl.ds(r, 128)] = e[pl.ds(r, 128), :].T
+        extra = stack_rows(split3(-lq_ref[pl.ds(i, 1), :]) + [1.0] * 6, 16)
+        e[pl.ds(r, 128), 128:256] = jnp.concatenate([extra, jnp.zeros((112, 128), F32)], axis=0).T.astype(BF16)
+        et[:, pl.ds(r, 128)] = e[pl.ds(r, 128), 0:128].T
         de_acc[pl.ds(r, 128), :] = jnp.zeros((128, 128), F32)
 
     ids[...] = lax.broadcasted_iota(jnp.int32, (SUB, 128), 0)
+    xa[144:256, :] = jnp.zeros((112, QB), BF16)
     t_acc[...] = jnp.zeros_like(t_acc)
     acc1[...] = jnp.zeros_like(acc1)
     acc2[...] = jnp.zeros_like(acc2)
-    drain(x_all.at[pl.ds(0, n - 1)], x_sem.at[1])
-    drain(lab_all.at[pl.ds(0, n - 1)], lab_sem.at[1])
+    pl.semaphore_wait(barrier, n - 1)
+
+    @pl.loop(1, chips)
+    def _(k):
+        to = peer(lax.rem(chip + k, chips) * 2 + core)
+        pltpu.make_async_remote_copy(x_mine, x_all.at[my_row], x_sem.at[0], x_sem.at[1], device_id=to, device_id_type=MESH).start()
+
+    drain(x_all.at[pl.ds(0, chips - 1)], x_sem.at[1])
+    swap_x = swap_cores(x_all, xs_sem)
+    swap_x.start()
+
+    @pl.loop(1, n)
+    def _(k):
+        pltpu.make_async_remote_copy(lab_mine, lab_all.at[my_row], lab_sem.at[0], lab_sem.at[1], device_id=peer(lax.rem(me + k, n)), device_id_type=MESH).start()
+
+    drain(x_all.at[pl.ds(0, chips)], xs_sem.at[1])
+
 
     def combine_stats(k):
         @pl.when(jnp.logical_and(my_k == k, my_j % half == 0))
@@ -125,25 +157,42 @@
                 pltpu.make_async_remote_copy(dx_mine, dx_all.at[my_slot], dxb_send, dxb_recv.at[k],
                                              device_id=peer(lax.rem(me + i, n)), device_id_type=MESH).start()
 
-    def logits(r):
-        lq = lqb[pl.ds(r, SUB), :]
-        z = jnp.dot(e[pl.ds(r, SUB), :], xbt[...], preferred_element_type=F32)
-        return z - jnp.concatenate([lq, lq], axis=1)
+    def logits(q):
+        return jnp.dot(e[pl.ds(pl.multiple_of(q * SUB, SUB), SUB), :], xa[...], preferred_element_type=F32)
+
+    chunks = items // SUB
+
+    def merge(tops, sums):
+        top = functools.reduce(jnp.maximum, tops)
+        return top, sum(s * jnp.exp2((m - top) * LOG2E) for m, s in zip(tops, sums))
+
+    def exp_sum(ref, m):
+        total = jnp.zeros((8, QB), F32)
+        for g in range(SUB // 8):
+            total = total + jnp.exp2((ref[8 * g:8 * g + 8, :] - m) * LOG2E)
+        return total
 
     @pl.loop(0, BLOCKS)
     def _(k):
-        xbt[...] = x_all[pl.ds(k * ob, ob)].reshape(QB, 128).T
+        xa[0:128, :] = x_all[pl.ds(row0(k), ob)].reshape(QB, 128).T
+        xa[128:144, :] = stack_rows([1.0] * 3, 16, QB).astype(BF16)
 
         def step(i, carry):
-            m, s = carry
+            m, s, m_last = carry
+            tops, sums = [m], [s]
             for u in range(UNROLL):
-                z = logits(pl.multiple_of((i * UNROLL + u) * SUB, SUB)).reshape(SUB // 8, 8, QB)
-                m_new = jnp.maximum(m, jnp.max(z, axis=0))
-                s = s * jnp.exp2((m - m_new) * LOG2E) + jnp.sum(jnp.exp2((z - m_new[None]) * LOG2E), axis=0)
-                m = m_new
-            return m, s
-
-        m, s = lax.fori_loop(0, items // (SUB * UNROLL), step, (jnp.full((8, QB), -3.0e38, F32), jnp.zeros((8, QB), F32)))
+                new, old = (za, zb) if u % 2 == 0 else (zb, za)
+                z = logits(i * UNROLL + u)
+                new[...] = z
+                tops.append(m_last)
+                sums.append(exp_sum(old, m_last))
+                m_last = functools.reduce(jnp.maximum, [z[8 * g:8 * g + 8, :] for g in range(SUB // 8)])
+            return merge(tops, sums) + (m_last,)
+
+        low = jnp.full((8, QB), LOW, F32)
+        zb[...] = jnp.full((SUB, QB), LOW, F32)
+        m, s, m_last = lax.fori_loop(0, chunks // UNROLL, step, (low, jnp.zeros((8, QB), F32), low))
+        m, s = merge([m, m_last], [s, exp_sum(zb, m_last)])
         top = jnp.max(m, axis=0, keepdims=True)
         total = jnp.sum(s * jnp.exp2((m - top) * LOG2E), axis=0, keepdims=True)
         for t in range(2):
@@ -161,7 +210,9 @@
 
         combine_stats(k - 4)
 
-    per_step = -(-(chips - 1) // (BLOCKS - 1))
+    drain(lab_all.at[pl.ds(0, n - 1)], lab_sem.at[1])
+    per_step = -(-(chips - 1) // (BLOCKS - 2))
+    swap_q = swap_cores(q_all, swap_sem)
 
     @pl.loop(0, BLOCKS)
     def _(k):
@@ -174,35 +225,62 @@
                 pltpu.make_async_remote_copy(q_ref, q_all.at[my_row], q_sem.at[0], q_sem.at[1],
                                              device_id=peer(lax.rem(chip + c, chips) * 2 + core), device_id_type=MESH).start()
 
+        @pl.when(k == BLOCKS - 1)
+        def _():
+            drain(q_all.at[pl.ds(0, chips - 1)], q_sem.at[1])
+            swap_q.start()
+
         for t in range(2):
             @pl.when(device_of(k, t * half, n) != me)
             def _():
                 drain(st_all.at[0], stb_recv.at[k * 2 + t])
 
-        xb = x_all[pl.ds(k * ob, ob)].reshape(QB, 128)
-        xbt[...] = xb.T
+        xb[...] = x_all[pl.ds(row0(k), ob)].reshape(QB, 128)
+        xa[0:128, :] = xb[...].T
         top = jnp.concatenate([st_all[k * 2, 0:1, :], st_all[k * 2 + 1, 0:1, :]], axis=1)
-        shift = jnp.concatenate([st_all[k * 2, 1:2, :], st_all[k * 2 + 1, 1:2, :]], axis=1) * LOG2E + math.log2(n * rows)
-        lab = jnp.concatenate([jnp.sum(lab_all[pl.ds(k * ob + t * half, half)], axis=0) for t in range(2)], axis=1) - me * items
+        norm = jnp.concatenate([st_all[k * 2, 1:2, :], st_all[k * 2 + 1, 1:2, :]], axis=1) + math.log(n * rows)
+        xa[128:144, :] = stack_rows([1.0] * 3 + split3(-top) + split3(-norm), 16, QB).astype(BF16)
+        lab = jnp.concatenate([jnp.sum(lab_all[pl.ds(row0(k) + t * half, half)], axis=0) for t in range(2)], axis=1) - me * items
         dxt[...] = jnp.zeros_like(dxt)
-
-        @pl.loop(0, items // (SUB * UNROLL))
+        gb[...] = jnp.zeros_like(gb)
+
+        zb[...] = jnp.full((SUB, QB), LOW, F32)
+        ga[...] = jnp.zeros_like(ga)
+
+        def spread(src, dst, q):
+            at = lab - jnp.where(q < 0, -(1 << 29), q * SUB)
+            at = jnp.broadcast_to(at, (8, QB))
+            tsum = t_acc[...]
+            for u in range(SUB // 16):
+                parts = []
+                for v in range(2):
+                    rows8 = pl.ds(u * 16 + v * 8, 8)
+                    z = src[rows8, :]
+                    idv = ids[rows8, :]
+                    hot = jnp.where(jnp.concatenate([idv, idv], axis=1) == at, 1.0 / (n * rows), 0.0)
+                    tsum = tsum + z * hot
+                    parts.append(jnp.exp2(z * LOG2E) - hot)
+                dst[u * 16:(u + 1) * 16, :] = jnp.concatenate(parts, axis=0).astype(BF16)
+            t_acc[...] = tsum
+
+        def gather(src, q):
+            r = pl.ds(pl.multiple_of(jnp.maximum(q, 0) * SUB, SUB), SUB)
+            de_acc[r, :] += jnp.dot(src[...], xb[...], preferred_element_type=F32)
+            dxt[...] += jnp.dot(et[:, r], src[...], preferred_element_type=F32)
+
+        @pl.loop(0, chunks // UNROLL)
         def _(i):
-            dx = dxt[...]
-            tsum = t_acc[...]
             for u in range(UNROLL):
-                r = pl.multiple_of((i * UNROLL + u) * SUB, SUB)
-                z = logits(r)
-                idv = ids[...]
-                hit = jnp.concatenate([idv, idv], axis=1) == lab - r
-                g = jnp.exp2((z - top) * LOG2E - shift) - jnp.where(hit, 1.0 / (n * rows), 0.0)
-                tsum = tsum + jnp.sum(jnp.where(hit, z, 0.0).reshape(SUB // 8, 8, QB), axis=0)
-                gb = g.astype(BF16)
-                de_acc[pl.ds(r, SUB), :] += jnp.dot(gb, xb, preferred_element_type=F32)
-                dx = dx + jnp.dot(et[:, pl.ds(r, SUB)], gb, preferred_element_type=F32)
-            dxt[...] = dx
-            t_acc[...] = tsum
-
+                q = i * UNROLL + u
+                new, old = (za, zb) if u % 2 == 0 else (zb, za)
+                here, gone = (gb, ga) if u % 2 == 0 else (ga, gb)
+                new[...] = logits(q)
+                spread(old, here, q - 1)
+                gather(gone, q - 2)
+
+        spread(zb, gb, chunks - 1)
+        gather(ga, chunks - 2)
+        gather(gb, chunks - 1)
         dx_part[pl.ds(k * ob, ob)] = dxt[...].T.reshape(ob, rows, 128)
 
         @pl.loop(0, ob)
@@ -230,21 +308,17 @@
     def _(i):
         pltpu.make_async_remote_copy(t_mine, t_all.at[me], t_sem.at[0], t_sem.at[1], device_id=peer(lax.rem(me + i, n)), device_id_type=MESH).start()
 
-    drain(q_all.at[pl.ds(0, chips - 1)], q_sem.at[1])
-    swap = pltpu.make_async_remote_copy(q_all.at[pl.ds(core * chips, chips)], q_all.at[pl.ds(core * chips, chips)], swap_sem.at[0], swap_sem.at[1], device_id=peer(chip * 2 + 1 - core), device_id_type=MESH)
-    swap.start()
-
-    @pl.loop(0, items // SUB)
+    @pl.loop(0, items // 512)
     def _(i):
-        r = pl.multiple_of(i * SUB, SUB)
-        de_out[pl.ds(r, SUB), :] = de_acc[pl.ds(r, SUB), :].astype(BF16)
+        r = pl.multiple_of(i * 512, 512)
+        de_out[pl.ds(r, 512), :] = de_acc[pl.ds(r, 512), :].astype(BF16)
 
     out = pltpu.make_async_copy(de_out, de_hbm, out_sem)
     out.start()
     drain(q_all.at[pl.ds(0, chips)], swap_sem.at[1])
 
     def rows_of(k):
-        return q_all[pl.ds((k % 2) * chips + (k // 2) * ob, ob)].reshape(QB, q_all.shape[-1])
+        return q_all[pl.ds(row0(k), ob)].reshape(QB, q_all.shape[-1])
 
     @pl.loop(0, BLOCKS)
     def _(k):
@@ -269,20 +343,18 @@
         acc1[...] += lax.dot_general(rows_of(k), da, (((0,), (0,)), ((), ())), preferred_element_type=F32)
 
     combine_rows(BLOCKS - 2)
-    pl.loop(0, BLOCKS - 3)(tower)
     combine_rows(BLOCKS - 1)
-    pl.loop(BLOCKS - 3, BLOCKS)(tower)
+    pl.loop(0, BLOCKS)(tower)
     dw1_ref[...] = acc1[...].astype(BF16)
     dw2_ref[...] = acc2[...].astype(BF16)
 
     drain(t_all.at[pl.ds(0, n - 1)], t_sem.at[1])
-    lse = st_all[:, 0:1, :] + st_all[:, 1:2, :]
-    total = jnp.sum(lse, axis=0) - jnp.sum(t_all[...], axis=0)
-    loss_ref[0] = jnp.sum(total) / (n * rows)
+    loss_ref[0] = -jnp.sum(t_all[...]) - math.log(n * rows)
 
     out.wait()
-    swap.wait_send()
-    drain(x_all.at[pl.ds(0, n - 1)], x_sem.at[0])
+    swap_q.wait_send()
+    swap_x.wait_send()
+    drain(x_all.at[pl.ds(0, chips - 1)], x_sem.at[0])
     drain(lab_all.at[pl.ds(0, n - 1)], lab_sem.at[0])
     drain(q_all.at[pl.ds(0, chips - 1)], q_sem.at[0])
     drain(t_all.at[pl.ds(0, n - 1)], t_sem.at[0])
@@ -319,12 +391,12 @@
             in_specs=[V, ANY, ANY, ANY, V, V],
             out_specs=(pl.BlockSpec(memory_space=pltpu.SMEM), ANY, V, V),
             scratch_shapes=[
-                M((width, hidden), BF16), M((hidden, 128), BF16), M((items, 128), BF16), M((128, items), BF16), M((items, 128), F32), M((SUB, 128), i32),
-                M((rows, 128), BF16), M((1, 128), i32), M((n, rows, 128), BF16), M((n, 1, 128), i32), M((n, rows, width), BF16), M((128, QB), BF16), M((8, 128), F32),
+                M((width, hidden), BF16), M((hidden, 128), BF16), M((items, 256), BF16), M((128, items), BF16), M((SUB, 128), i32),
+                M((rows, 128), BF16), M((1, 128), i32), M((n, rows, 128), BF16), M((n, 1, 128), i32), M((n, rows, width), BF16), M((256, QB), BF16), M((QB, 128), BF16), M((SUB, QB), F32), M((SUB, QB), F32), M((SUB, QB), BF16), M((SUB, QB), BF16),
                 M((2 * BLOCKS, 2, 128), F32), M((n, 2, 128), F32), M((2, 128), F32), M((2 * BLOCKS, 2, 128), F32), M((items, 128), F32), M((items, 128), BF16), M((128, QB), F32),
                 M((n, rows, 128), F32), M((n, rows, 128), F32), M((rows, 128), BF16), M((n, rows, 128), BF16),
                 M((8, QB), F32), M((1, 128), F32), M((n, 1, 128), F32), M((BLOCKS, QB, hidden), F32), M((width, hidden), F32), M((hidden, 128), F32),
-                DMA((3,)), DMA, DMA((2,)), DMA((2,)), DMA((2,)), DMA((2,)), DMA((2,)), DMA, DMA((2 * BLOCKS,)), DMA((2,)), DMA, DMA((BLOCKS,)), DMA((2,)),
+                DMA((3,)), DMA, DMA((2,)), DMA((2,)), DMA((2,)), DMA((2,)), DMA((2,)), DMA((2,)), DMA, DMA((2 * BLOCKS,)), DMA((2,)), DMA, DMA((BLOCKS,)), DMA((2,)),
             ],
             compiler_params=pltpu.CompilerParams(collective_id=0, has_side_effects=True, vmem_limit_bytes=60 << 20),
         )(queries, w_first, w_second, catalogue, log_q.reshape(items // 128, 128), labels.reshape(1, rows))

time: 125 us -> 113 us (0.904)
  Pallas kernels: 118 us -> 105 us
    pallas_call x1, Pallas kernels: 118 us -> 105 us  [local_step(): pl.pallas_call(functools.partial(kernel, n, rows, items), name='two_tower...]
where the time goes in v3:
time: 113 us; the launch traced here: 112 us
  Pallas kernels  105 us (93%)
  local copies, waits for them, and re-layouts  4.94 us (4%)
  between operations  2.4 us (2%)
    pallas_call x1, Pallas kernels, local_step(): pl.pallas_call(functools.partial(kernel, n, rows, items), name='two_tower...  105 us
    unnamed x7, local copies, waits for them, and re-layouts  4.94 us

profile of v3, /device:TPU:1, one launch (start us, length us, event | category | flops | bytes accessed | tf_op | source)
XLA Modules:
  0.0 112.3 jit_solution(15421286649450320914)
XLA Ops:
  0.6 105.0 %two_tower.1 = (f32[1]{0:T(128)}, bf16[8192,128]{1,0:T(8,128)(2,1)}, bf16[768,768]{1,0:T(8,128)(2,1)}, bf16[768,128]{1,0:T(8,128)(2,1)}) custom-call(bf16[16,768]{1,0:T(8,128)(2,1)} %q_ref.1, bf16[768,768]{1,0:T(8,128)(2,1)} %w1_hbm.1, bf16[768,128]{1,0:T(8,128)(2,1)} %w2_hbm.1, bf16[8192,128]{1,0:T(8,128)(2,1)} %e_hbm.1, f32[64,128]{1,0:T(8,128)} %bitcast.2, ...), custom_call_target="tpu_custom_call" | custom-call | tf_op jit(solution)/shard_map/two_tower/pallas_call | solution.py:387
  106.2 0.0 copy-start
  106.2 3.1 %copy.15 = bf16[8192,128]{1,0:T(8,128)(2,1)} copy(bf16[8192,128]{1,0:T(8,128)(2,1)} %get-tuple-element.9) | data formatting | bytes 4194304
  109.4 0.0 copy-done
  109.4 0.0 copy-start.1
  109.4 1.0 copy.16
  110.4 0.1 copy-done.1
  110.5 0.7 copy.17
Async XLA Ops:
  106.2 3.2 %copy-start = (bf16[768,768]{1,0:T(8,128)(2,1)S(1)}, bf16[768,768]{1,0:T(8,128)(2,1)}, u32[]{:S(2)}) copy-start(bf16[768,768]{1,0:T(8,128)(2,1)} %get-tuple-element.10) | copy-start | bytes 3538948
  109.4 1.1 copy-start.1

commit v4 on v3

--- a/solution.py
+++ b/solution.py
@@ -61,9 +61,9 @@
            q_ref, w1_hbm, w2_hbm, e_hbm, lq_ref, lab_ref,
            loss_ref, de_hbm, dw1_ref, dw2_ref,
            w1, w2, e, et, ids, x_mine, lab_mine, x_all, lab_all, q_all, xa, xb, za, zb, ga, gb,
-           st_send, st_got, st_mine, st_all, de_acc, de_out, dxt, dx_part, dx_got, dx_mine, dx_all,
+           st_send, st_got, st_mine, st_all, de_acc, de_out, dxt, dx_part, pair, dx_sum, dx_got, dx_mine, dx_all,
            t_acc, t_mine, t_all, pre, acc1, acc2,
-           load_sem, out_sem, x_sem, xs_sem, lab_sem, q_sem, swap_sem, st_sem, stb_send, stb_recv, dx_sem, dxb_send, dxb_recv, t_sem):
+           load_sem, out_sem, x_sem, xs_sem, lab_sem, q_sem, swap_sem, st_sem, stb_send, stb_recv, pair_send, pair_recv, dx_sem, dxb_send, dxb_recv, t_sem):
     me = lax.axis_index("tp")
     ob = n // BLOCKS
     half = ob // 2
@@ -100,13 +100,15 @@
     q_all[pl.ds(my_row, 1)] = q_ref[...][None]
     loads[2].wait()
 
-    @pl.loop(0, items // 128)
+    @pl.loop(0, items // 1024)
     def _(i):
-        r = pl.multiple_of(i * 128, 128)
-        extra = stack_rows(split3(-lq_ref[pl.ds(i, 1), :]) + [1.0] * 6, 16)
-        e[pl.ds(r, 128), 128:256] = jnp.concatenate([extra, jnp.zeros((112, 128), F32)], axis=0).T.astype(BF16)
-        et[:, pl.ds(r, 128)] = e[pl.ds(r, 128), 0:128].T
-        de_acc[pl.ds(r, 128), :] = jnp.zeros((128, 128), F32)
+        parts = split3(-lq_ref[pl.ds(pl.multiple_of(i * 8, 8), 8), :])
+        for u in range(8):
+            r = pl.multiple_of(i * 1024 + u * 128, 128)
+            extra = stack_rows([p[u:u + 1, :] for p in parts] + [1.0] * 6, 16)
+            e[pl.ds(r, 128), 128:256] = jnp.concatenate([extra, jnp.zeros((112, 128), F32)], axis=0).T.astype(BF16)
+            et[:, pl.ds(r, 128)] = e[pl.ds(r, 128), 0:128].T
+            de_acc[pl.ds(r, 128), :] = jnp.zeros((128, 128), F32)
 
     ids[...] = lax.broadcasted_iota(jnp.int32, (SUB, 128), 0)
     xa[144:256, :] = jnp.zeros((112, QB), BF16)
@@ -145,10 +147,35 @@
                 pltpu.make_async_remote_copy(st_mine, st_all.at[k * 2 + my_j // half], stb_send, stb_recv.at[k * 2 + my_j // half],
                                              device_id=peer(lax.rem(me + i, n)), device_id_type=MESH).start()
 
+    def flush(k):
+        drain(pair.at[pl.ds(0, half)], pair_recv.at[k])
+        dx_sum[pl.ds(k * half, half)] = dx_part[pl.ds(k * ob + core * half, half)] + pair[pl.ds(k * half, half)]
+
+        @pl.loop(0, half)
+        def _(j):
+            to = device_of(k, core * half + j, n)
+
+            @pl.when(to != me)
+            def _():
+                pltpu.make_async_remote_copy(dx_sum.at[k * half + j], dx_got.at[chip], dx_sem.at[0], dx_sem.at[1], device_id=peer(to), device_id_type=MESH).start()
+
+            @pl.when(to == me)
+            def _():
+                dx_got[pl.ds(chip, 1)] = dx_sum[pl.ds(k * half + j, 1)]
+
+    own_half = my_j // half == core
+
     def combine_rows(k):
         @pl.when(my_k == k)
         def _():
-            drain(dx_got.at[pl.ds(0, n - 1)], dx_sem.at[1])
+            @pl.when(own_half)
+            def _():
+                drain(dx_got.at[pl.ds(0, chips - 1)], dx_sem.at[1])
+
+            @pl.when(jnp.logical_not(own_half))
+            def _():
+                drain(dx_got.at[pl.ds(0, chips)], dx_sem.at[1])
+
             dx_mine[...] = jnp.sum(dx_got[...], axis=0).astype(BF16)
             dx_all[pl.ds(my_slot, 1)] = dx_mine[...][None]
 
@@ -171,6 +198,18 @@
         for g in range(SUB // 8):
             total = total + jnp.exp2((ref[8 * g:8 * g + 8, :] - m) * LOG2E)
         return total
+
+    per_step = -(-(chips - 1) // (2 * BLOCKS - 2))
+
+    def send_rows(step):
+        @pl.loop(0, per_step)
+        def _(i):
+            c = step * per_step + i + 1
+
+            @pl.when(c < chips)
+            def _():
+                pltpu.make_async_remote_copy(q_ref, q_all.at[my_row], q_sem.at[0], q_sem.at[1],
+                                             device_id=peer(lax.rem(chip + c, chips) * 2 + core), device_id_type=MESH).start()
 
     @pl.loop(0, BLOCKS)
     def _(k):
@@ -208,22 +247,15 @@
             def _():
                 st_got[pl.ds(me, 1)] = st_send[pl.ds(k * 2 + t, 1)]
 
+        send_rows(k)
         combine_stats(k - 4)
 
     drain(lab_all.at[pl.ds(0, n - 1)], lab_sem.at[1])
-    per_step = -(-(chips - 1) // (BLOCKS - 2))
     swap_q = swap_cores(q_all, swap_sem)
 
     @pl.loop(0, BLOCKS)
     def _(k):
-        @pl.loop(0, per_step)
-        def _(i):
-            c = k * per_step + i + 1
-
-            @pl.when(c < chips)
-            def _():
-                pltpu.make_async_remote_copy(q_ref, q_all.at[my_row], q_sem.at[0], q_sem.at[1],
-                                             device_id=peer(lax.rem(chip + c, chips) * 2 + core), device_id_type=MESH).start()
+        send_rows(BLOCKS + k)
 
         @pl.when(k == BLOCKS - 1)
         def _():
@@ -278,28 +310,23 @@
                 spread(old, here, q - 1)
                 gather(gone, q - 2)
 
+        @pl.when(k > 0)
+        def _():
+            flush(k - 1)
+
         spread(zb, gb, chunks - 1)
         gather(ga, chunks - 2)
         gather(gb, chunks - 1)
         dx_part[pl.ds(k * ob, ob)] = dxt[...].T.reshape(ob, rows, 128)
 
-        @pl.loop(0, ob)
-        def _(j):
-            to = device_of(k, j, n)
-
-            @pl.when(to != me)
-            def _():
-                pltpu.make_async_remote_copy(dx_part.at[k * ob + j], dx_got.at[me], dx_sem.at[0], dx_sem.at[1], device_id=peer(to), device_id_type=MESH).start()
-
-            @pl.when(to == me)
-            def _():
-                dx_got[pl.ds(me, 1)] = dx_part[pl.ds(k * ob + j, 1)]
+        pltpu.make_async_remote_copy(dx_part.at[pl.ds(k * ob + (1 - core) * half, half)], pair.at[pl.ds(k * half, half)], pair_send, pair_recv.at[k],
+                                     device_id=peer(chip * 2 + 1 - core), device_id_type=MESH).start()
 
         @pl.when(k < 4)
         def _():
             combine_stats(k + 4)
 
-        combine_rows(k - 2)
+        combine_rows(k - 3)
 
     t_mine[...] = jnp.sum(t_acc[:, 0:128] + t_acc[:, 128:256], axis=0, keepdims=True)
     t_all[pl.ds(me, 1)] = t_mine[...][None]
@@ -307,6 +334,8 @@
     @pl.loop(1, n)
     def _(i):
         pltpu.make_async_remote_copy(t_mine, t_all.at[me], t_sem.at[0], t_sem.at[1], device_id=peer(lax.rem(me + i, n)), device_id_type=MESH).start()
+
+    flush(BLOCKS - 1)
 
     @pl.loop(0, items // 512)
     def _(i):
@@ -342,6 +371,7 @@
         da = jnp.where(a > 0.0, dh, 0.0).astype(BF16)
         acc1[...] += lax.dot_general(rows_of(k), da, (((0,), (0,)), ((), ())), preferred_element_type=F32)
 
+    combine_rows(BLOCKS - 3)
     combine_rows(BLOCKS - 2)
     combine_rows(BLOCKS - 1)
     pl.loop(0, BLOCKS)(tower)
@@ -358,7 +388,15 @@
     drain(lab_all.at[pl.ds(0, n - 1)], lab_sem.at[0])
     drain(q_all.at[pl.ds(0, chips - 1)], q_sem.at[0])
     drain(t_all.at[pl.ds(0, n - 1)], t_sem.at[0])
-    drain(dx_got.at[pl.ds(0, n - 1)], dx_sem.at[0])
+    drain(pair.at[pl.ds(0, BLOCKS * half)], pair_send)
+
+    @pl.when(own_half)
+    def _():
+        drain(dx_got.at[pl.ds(0, chips - 1)], dx_sem.at[0])
+
+    @pl.when(jnp.logical_not(own_half))
+    def _():
+        drain(dx_got.at[pl.ds(0, chips)], dx_sem.at[0])
 
     @pl.when(my_j % half == 0)
     def _():
@@ -394,9 +432,9 @@
                 M((width, hidden), BF16), M((hidden, 128), BF16), M((items, 256), BF16), M((128, items), BF16), M((SUB, 128), i32),
                 M((rows, 128), BF16), M((1, 128), i32), M((n, rows, 128), BF16), M((n, 1, 128), i32), M((n, rows, width), BF16), M((256, QB), BF16), M((QB, 128), BF16), M((SUB, QB), F32), M((SUB, QB), F32), M((SUB, QB), BF16), M((SUB, QB), BF16),
                 M((2 * BLOCKS, 2, 128), F32), M((n, 2, 128), F32), M((2, 128), F32), M((2 * BLOCKS, 2, 128), F32), M((items, 128), F32), M((items, 128), BF16), M((128, QB), F32),
-                M((n, rows, 128), F32), M((n, rows, 128), F32), M((rows, 128), BF16), M((n, rows, 128), BF16),
+                M((n, rows, 128), F32), M((n // 2, rows, 128), F32), M((n // 2, rows, 128), F32), M((n // 2, rows, 128), F32), M((rows, 128), BF16), M((n, rows, 128), BF16),
                 M((8, QB), F32), M((1, 128), F32), M((n, 1, 128), F32), M((BLOCKS, QB, hidden), F32), M((width, hidden), F32), M((hidden, 128), F32),
-                DMA((3,)), DMA, DMA((2,)), DMA((2,)), DMA((2,)), DMA((2,)), DMA((2,)), DMA((2,)), DMA, DMA((2 * BLOCKS,)), DMA((2,)), DMA, DMA((BLOCKS,)), DMA((2,)),
+                DMA((3,)), DMA, DMA((2,)), DMA((2,)), DMA((2,)), DMA((2,)), DMA((2,)), DMA((2,)), DMA, DMA((2 * BLOCKS,)), DMA, DMA((BLOCKS,)), DMA((2,)), DMA, DMA((BLOCKS,)), DMA((2,)),
             ],
             compiler_params=pltpu.CompilerParams(collective_id=0, has_side_effects=True, vmem_limit_bytes=60 << 20),
         )(queries, w_first, w_second, catalogue, log_q.reshape(items // 128, 128), labels.reshape(1, rows))

time: 113 us -> 102 us (0.903)
  Pallas kernels: 105 us -> 94.1 us
    pallas_call x1, Pallas kernels: 105 us -> 94.1 us  [local_step(): pl.pallas_call(functools.partial(kernel, n, rows, items), name='two_tower...]
where the time goes in v4:
time: 102 us; the launch traced here: 101 us
  Pallas kernels  94.1 us (92%)
  local copies, waits for them, and re-layouts  4.94 us (5%)
  between operations  2.4 us (2%)
    pallas_call x1, Pallas kernels, local_step(): pl.pallas_call(functools.partial(kernel, n, rows, items), name='two_tower...  94.1 us
    unnamed x7, local copies, waits for them, and re-layouts  4.94 us

profile of v4, /device:TPU:1, one launch (start us, length us, event | category | flops | bytes accessed | tf_op | source)
XLA Modules:
  0.0 101.4 jit_solution(17858099040574173720)
XLA Ops:
  0.6 94.1 %two_tower.1 = (f32[1]{0:T(128)}, bf16[8192,128]{1,0:T(8,128)(2,1)}, bf16[768,768]{1,0:T(8,128)(2,1)}, bf16[768,128]{1,0:T(8,128)(2,1)}) custom-call(bf16[16,768]{1,0:T(8,128)(2,1)} %q_ref.1, bf16[768,768]{1,0:T(8,128)(2,1)} %w1_hbm.1, bf16[768,128]{1,0:T(8,128)(2,1)} %w2_hbm.1, bf16[8192,128]{1,0:T(8,128)(2,1)} %e_hbm.1, f32[64,128]{1,0:T(8,128)} %bitcast.2, ...), custom_call_target="tpu_custom_call" | custom-call | tf_op jit(solution)/shard_map/two_tower/pallas_call | solution.py:425
  95.3 0.0 copy-start
  95.3 3.1 %copy.15 = bf16[8192,128]{1,0:T(8,128)(2,1)} copy(bf16[8192,128]{1,0:T(8,128)(2,1)} %get-tuple-element.9) | data formatting | bytes 4194304
  98.5 0.0 copy-done
  98.5 0.0 copy-start.1
  98.5 1.0 copy.16
  99.5 0.1 copy-done.1
  99.6 0.7 copy.17
Async XLA Ops:
  95.3 3.2 %copy-start = (bf16[768,768]{1,0:T(8,128)(2,1)S(1)}, bf16[768,768]{1,0:T(8,128)(2,1)}, u32[]{:S(2)}) copy-start(bf16[768,768]{1,0:T(8,128)(2,1)} %get-tuple-element.10) | copy-start | bytes 3538948
  98.5 1.1 %copy-start.1 = (bf16[768,128]{1,0:T(8,128)(2,1)S(1)}, bf16[768,128]{1,0:T(8,128)(2,1)}, u32[]{:S(2)}) copy-start(bf16[768,128]{1,0:T(8,128)(2,1)} %get-tuple-element.11) | copy-start | bytes 589828

commit v5 on v4

--- a/solution.py
+++ b/solution.py
@@ -55,6 +55,10 @@
     for i, v in enumerate(values):
         out = jnp.where(at == i, v, out)
     return out
+
+
+def stat_owner(k, t, n):
+    return device_of(5, 2 * k + t, n) if n == 128 else device_of(k, t * (n // BLOCKS // 2), n)
 
 
 def kernel(n, rows, items,
@@ -72,6 +76,11 @@
     core, chip, chips = me % 2, me // 2, n // 2
     my_row = core * chips + (my_k // 2) * ob + my_j
 
+    if n == 128:
+        is_stat, stat_k, stat_t = my_k == 5, my_j // 2, my_j % 2
+    else:
+        is_stat, stat_k, stat_t = my_j % half == 0, my_k, my_j // half
+
     def row0(k):
         return (k % 2) * chips + (k // 2) * ob
 
@@ -134,17 +143,17 @@
 
 
     def combine_stats(k):
-        @pl.when(jnp.logical_and(my_k == k, my_j % half == 0))
+        @pl.when(jnp.logical_and(is_stat, stat_k == k))
         def _():
             drain(st_got.at[pl.ds(0, n - 1)], st_sem.at[1])
             top = jnp.max(st_got[:, 0:1, :], axis=0)
             total = jnp.sum(st_got[:, 1:2, :] * jnp.exp(st_got[:, 0:1, :] - top[None]), axis=0)
             st_mine[...] = jnp.concatenate([top, jnp.log(total)], axis=0)
-            st_all[pl.ds(k * 2 + my_j // half, 1)] = st_mine[...][None]
+            st_all[pl.ds(k * 2 + stat_t, 1)] = st_mine[...][None]
 
             @pl.loop(1, n)
             def _(i):
-                pltpu.make_async_remote_copy(st_mine, st_all.at[k * 2 + my_j // half], stb_send, stb_recv.at[k * 2 + my_j // half],
+                pltpu.make_async_remote_copy(st_mine, st_all.at[k * 2 + stat_t], stb_send, stb_recv.at[k * 2 + stat_t],
                                              device_id=peer(lax.rem(me + i, n)), device_id_type=MESH).start()
 
     def flush(k):
@@ -237,7 +246,7 @@
         for t in range(2):
             st_send[pl.ds(k * 2 + t, 1)] = jnp.concatenate([top[:, t * 128:(t + 1) * 128], total[:, t * 128:(t + 1) * 128]], axis=0)[None]
         for t in range(2):
-            to = device_of(k, t * half, n)
+            to = stat_owner(k, t, n)
 
             @pl.when(to != me)
             def _():
@@ -248,7 +257,7 @@
                 st_got[pl.ds(me, 1)] = st_send[pl.ds(k * 2 + t, 1)]
 
         send_rows(k)
-        combine_stats(k - 4)
+        combine_stats(jnp.where(k == BLOCKS - 1, 2, jnp.where(k < 6, k - 4, -1)))
 
     drain(lab_all.at[pl.ds(0, n - 1)], lab_sem.at[1])
     swap_q = swap_cores(q_all, swap_sem)
@@ -263,7 +272,7 @@
             swap_q.start()
 
         for t in range(2):
-            @pl.when(device_of(k, t * half, n) != me)
+            @pl.when(stat_owner(k, t, n) != me)
             def _():
                 drain(st_all.at[0], stb_recv.at[k * 2 + t])
 
@@ -310,10 +319,6 @@
                 spread(old, here, q - 1)
                 gather(gone, q - 2)
 
-        @pl.when(k > 0)
-        def _():
-            flush(k - 1)
-
         spread(zb, gb, chunks - 1)
         gather(ga, chunks - 2)
         gather(gb, chunks - 1)
@@ -322,9 +327,11 @@
         pltpu.make_async_remote_copy(dx_part.at[pl.ds(k * ob + (1 - core) * half, half)], pair.at[pl.ds(k * half, half)], pair_send, pair_recv.at[k],
                                      device_id=peer(chip * 2 + 1 - core), device_id_type=MESH).start()
 
-        @pl.when(k < 4)
-        def _():
-            combine_stats(k + 4)
+        @pl.when(k > 0)
+        def _():
+            flush(k - 1)
+
+        combine_stats(k + 3)
 
         combine_rows(k - 3)
 
@@ -398,16 +405,50 @@
     def _():
         drain(dx_got.at[pl.ds(0, chips)], dx_sem.at[0])
 
-    @pl.when(my_j % half == 0)
+    @pl.when(is_stat)
     def _():
         drain(st_got.at[pl.ds(0, n - 1)], stb_send)
         drain(st_got.at[pl.ds(0, 2 * BLOCKS - 1)], st_sem.at[0])
 
-    @pl.when(my_j % half != 0)
+    @pl.when(jnp.logical_not(is_stat))
     def _():
         drain(st_got.at[pl.ds(0, 2 * BLOCKS)], st_sem.at[0])
 
     drain(dx_all.at[pl.ds(0, n - 1)], dxb_send)
+
+
+def store_kernel(pieces, *refs):
+    count = len(pieces)
+    ins, outs, bufs, in_sem, out_sem = refs[:count], refs[count:2 * count], refs[2 * count:3 * count], refs[-2], refs[-1]
+    reads, writes = [], []
+    for a, o, v, p in zip(ins, outs, bufs, pieces):
+        step = a.shape[0] // p
+        for i in range(p):
+            part = pl.ds(i * step, step)
+            at = len(reads)
+            reads.append(pltpu.make_async_copy(a.at[part], v.at[part], in_sem.at[at]))
+            writes.append(pltpu.make_async_copy(v.at[part], o.at[part], out_sem.at[at]))
+    for c in reads:
+        c.start()
+    for r, w in zip(reads, writes):
+        r.wait()
+        w.start()
+    for w in writes:
+        w.wait()
+
+
+def store(*arrays):
+    pieces = (4, 2, 1)
+    any_space = pl.BlockSpec(memory_space=pl.ANY)
+    return pl.pallas_call(
+        functools.partial(store_kernel, pieces),
+        name="store",
+        out_shape=tuple(jax.ShapeDtypeStruct(a.shape, a.dtype) for a in arrays),
+        in_specs=[any_space] * 3,
+        out_specs=(any_space,) * 3,
+        scratch_shapes=[pltpu.VMEM(a.shape, a.dtype) for a in arrays] + [DMA((sum(pieces),)), DMA((sum(pieces),))],
+        compiler_params=pltpu.CompilerParams(vmem_limit_bytes=60 << 20),
+    )(*arrays)
 
 
 def solution(mesh):
@@ -438,7 +479,7 @@
             ],
             compiler_params=pltpu.CompilerParams(collective_id=0, has_side_effects=True, vmem_limit_bytes=60 << 20),
         )(queries, w_first, w_second, catalogue, log_q.reshape(items // 128, 128), labels.reshape(1, rows))
-        return loss, grad_items, grad_first, grad_second
+        return (loss,) + tuple(store(grad_items, grad_first, grad_second))
 
     row_spec = P(("dp", "tp"), None)
     return jax.shard_map(local_step, mesh=mesh, in_specs=(row_spec, P(None, None), P(None, None), P("tp", None), P("tp"), P(("dp", "tp"))), out_specs=(P("dp"), row_spec, P("dp", None), P("dp", None)), check_vma=False)

time: 102 us -> 96.3 us (0.944)
  local copies, waits for them, and re-layouts: 4.94 us -> 0 us
    unnamed x7 -> x0, local copies, waits for them, and re-layouts: 4.94 us -> none
    pallas_call x1, Pallas kernels: 94.1 us -> 90.8 us  [local_step(): pl.pallas_call(functools.partial(kernel, n, rows, items), name='two_tower...]
    pallas_call x0 -> x1, Pallas kernels: none -> 2.92 us  [store(): pl.pallas_call(functools.partial(store_kernel, pieces), name='store', out...]
where the time goes in v5:
time: 96.3 us; the launch traced here: 96.1 us
  Pallas kernels  93.7 us (97%)
  between operations  2.41 us (3%)
    pallas_call x1, Pallas kernels, local_step(): pl.pallas_call(functools.partial(kernel, n, rows, items), name='two_tower...  90.8 us
    pallas_call x1, Pallas kernels, store(): pl.pallas_call(functools.partial(store_kernel, pieces), name='store', out...  2.92 us

profile of v5, /device:TPU:1, one launch (start us, length us, event | category | flops | bytes accessed | tf_op | source)
XLA Modules:
  0.0 96.1 jit_solution(15287328084141858587)
XLA Ops:
  0.6 90.8 %two_tower.1 = (f32[1]{0:T(128)}, bf16[8192,128]{1,0:T(8,128)(2,1)}, bf16[768,768]{1,0:T(8,128)(2,1)}, bf16[768,128]{1,0:T(8,128)(2,1)}) custom-call(bf16[16,768]{1,0:T(8,128)(2,1)} %q_ref.1, bf16[768,768]{1,0:T(8,128)(2,1)} %w1_hbm.1, bf16[768,128]{1,0:T(8,128)(2,1)} %w2_hbm.1, bf16[8192,128]{1,0:T(8,128)(2,1)} %e_hbm.1, f32[64,128]{1,0:T(8,128)} %bitcast.2, ...), custom_call_target="tpu_custom_call" | custom-call | tf_op jit(solution)/shard_map/two_tower/pallas_call | solution.py:466
  91.4 2.9 %store.1 = (bf16[8192,128]{1,0:T(8,128)(2,1)}, bf16[768,768]{1,0:T(8,128)(2,1)}, bf16[768,128]{1,0:T(8,128)(2,1)}) custom-call(bf16[8192,128]{1,0:T(8,128)(2,1)} %get-tuple-element.12.refs_0_, bf16[768,768]{1,0:T(8,128)(2,1)} %get-tuple-element.13.refs_1_, bf16[768,128]{1,0:T(8,128)(2,1)} %get-tuple-element.14.refs_2_), custom_call_target="tpu_custom_call" | custom-call | tf_op jit(solution)/shard_map/store/pallas_call | solution.py:443

commit v6 on v5

--- a/solution.py
+++ b/solution.py
@@ -12,10 +12,9 @@
 F32, BF16 = jnp.float32, jnp.bfloat16
 LOG2E = 1.4426950408889634
 BLOCKS = 8
-LOW = -3.0e38
 QB = 256
 SUB = 512
-UNROLL = 16
+KEEP = 3
 
 
 def peer(index):
@@ -42,6 +41,18 @@
     return (j * 4 + k // 2) * 2 + k % 2
 
 
+def each(first, count, f):
+    steps = (count - first) // 4
+
+    @pl.loop(0, steps)
+    def _(s):
+        for u in range(4):
+            f(first + s * 4 + u)
+
+    for i in range(first + steps * 4, count):
+        f(i)
+
+
 def split3(v):
     big = float(jnp.finfo(BF16).max)
     a = jnp.clip(v, -big, big).astype(BF16).astype(F32)
@@ -64,7 +75,7 @@
 def kernel(n, rows, items,
            q_ref, w1_hbm, w2_hbm, e_hbm, lq_ref, lab_ref,
            loss_ref, de_hbm, dw1_ref, dw2_ref,
-           w1, w2, e, et, ids, x_mine, lab_mine, x_all, lab_all, q_all, xa, xb, za, zb, ga, gb,
+           w1, w2, e, et, ids, x_mine, lab_mine, x_all, lab_all, q_all, xa, xb, za, zb, ga, gb, keep, xk,
            st_send, st_got, st_mine, st_all, de_acc, de_out, dxt, dx_part, pair, dx_sum, dx_got, dx_mine, dx_all,
            t_acc, t_mine, t_all, pre, acc1, acc2,
            load_sem, out_sem, x_sem, xs_sem, lab_sem, q_sem, swap_sem, st_sem, stb_send, stb_recv, pair_send, pair_recv, dx_sem, dxb_send, dxb_recv, t_sem):
@@ -93,9 +104,7 @@
         c.start()
     barrier = pltpu.get_barrier_semaphore()
 
-    @pl.loop(1, n)
-    def _(k):
-        pl.semaphore_signal(barrier, inc=1, device_id=peer(lax.rem(me + k, n)), device_id_type=MESH)
+    each(1, n, lambda k: pl.semaphore_signal(barrier, inc=1, device_id=peer(lax.rem(me + k, n)), device_id_type=MESH))
 
     loads[0].wait()
     loads[1].wait()
@@ -126,19 +135,19 @@
     acc2[...] = jnp.zeros_like(acc2)
     pl.semaphore_wait(barrier, n - 1)
 
-    @pl.loop(1, chips)
-    def _(k):
+    def send_x(k):
         to = peer(lax.rem(chip + k, chips) * 2 + core)
         pltpu.make_async_remote_copy(x_mine, x_all.at[my_row], x_sem.at[0], x_sem.at[1], device_id=to, device_id_type=MESH).start()
 
+    def send_labels(k):
+        to = peer(lax.rem(me + k, n))
+        pltpu.make_async_remote_copy(lab_mine, lab_all.at[my_row], lab_sem.at[0], lab_sem.at[1], device_id=to, device_id_type=MESH).start()
+
+    each(1, chips, send_x)
+    each(1, n, send_labels)
     drain(x_all.at[pl.ds(0, chips - 1)], x_sem.at[1])
     swap_x = swap_cores(x_all, xs_sem)
     swap_x.start()
-
-    @pl.loop(1, n)
-    def _(k):
-        pltpu.make_async_remote_copy(lab_mine, lab_all.at[my_row], lab_sem.at[0], lab_sem.at[1], device_id=peer(lax.rem(me + k, n)), device_id_type=MESH).start()
-
     drain(x_all.at[pl.ds(0, chips)], xs_sem.at[1])
 
 
@@ -151,10 +160,11 @@
             st_mine[...] = jnp.concatenate([top, jnp.log(total)], axis=0)
             st_all[pl.ds(k * 2 + stat_t, 1)] = st_mine[...][None]
 
-            @pl.loop(1, n)
-            def _(i):
+            def send(i):
                 pltpu.make_async_remote_copy(st_mine, st_all.at[k * 2 + stat_t], stb_send, stb_recv.at[k * 2 + stat_t],
                                              device_id=peer(lax.rem(me + i, n)), device_id_type=MESH).start()
+
+            each(1, n, send)
 
     def flush(k):
         drain(pair.at[pl.ds(0, half)], pair_recv.at[k])
@@ -188,13 +198,14 @@
             dx_mine[...] = jnp.sum(dx_got[...], axis=0).astype(BF16)
             dx_all[pl.ds(my_slot, 1)] = dx_mine[...][None]
 
-            @pl.loop(1, n)
-            def _(i):
+            def send(i):
                 pltpu.make_async_remote_copy(dx_mine, dx_all.at[my_slot], dxb_send, dxb_recv.at[k],
                                              device_id=peer(lax.rem(me + i, n)), device_id_type=MESH).start()
 
+            each(1, n, send)
+
     def logits(q):
-        return jnp.dot(e[pl.ds(pl.multiple_of(q * SUB, SUB), SUB), :], xa[...], preferred_element_type=F32)
+        return jnp.dot(e[pl.ds(q * SUB, SUB), :], xa[...], preferred_element_type=F32)
 
     chunks = items // SUB
 
@@ -204,8 +215,9 @@
 
     def exp_sum(ref, m):
         total = jnp.zeros((8, QB), F32)
-        for g in range(SUB // 8):
-            total = total + jnp.exp2((ref[8 * g:8 * g + 8, :] - m) * LOG2E)
+        for g in range(SUB // 64):
+            z = ref[64 * g:64 * g + 64, :].reshape(8, 8, QB)
+            total = total + jnp.sum(jnp.exp2((z - m[None]) * LOG2E), axis=0)
         return total
 
     per_step = -(-(chips - 1) // (2 * BLOCKS - 2))
@@ -225,22 +237,22 @@
         xa[0:128, :] = x_all[pl.ds(row0(k), ob)].reshape(QB, 128).T
         xa[128:144, :] = stack_rows([1.0] * 3, 16, QB).astype(BF16)
 
-        def step(i, carry):
-            m, s, m_last = carry
-            tops, sums = [m], [s]
-            for u in range(UNROLL):
-                new, old = (za, zb) if u % 2 == 0 else (zb, za)
-                z = logits(i * UNROLL + u)
+        m = s = None
+        tops, sums = [], []
+        for q in range(chunks + 1):
+            new, old = (za, zb) if q % 2 == 0 else (zb, za)
+            if q < chunks:
+                z = logits(q)
                 new[...] = z
-                tops.append(m_last)
-                sums.append(exp_sum(old, m_last))
-                m_last = functools.reduce(jnp.maximum, [z[8 * g:8 * g + 8, :] for g in range(SUB // 8)])
-            return merge(tops, sums) + (m_last,)
-
-        low = jnp.full((8, QB), LOW, F32)
-        zb[...] = jnp.full((SUB, QB), LOW, F32)
-        m, s, m_last = lax.fori_loop(0, chunks // UNROLL, step, (low, jnp.zeros((8, QB), F32), low))
-        m, s = merge([m, m_last], [s, exp_sum(zb, m_last)])
+            if q > 0:
+                sums.append(exp_sum(old, tops[len(sums)]))
+            if q < chunks:
+                tops.append(jnp.max(z.reshape(SUB // 8, 8, QB), axis=0))
+            if len(sums) == 4 or q == chunks:
+                done = len(sums)
+                old_parts = ([m], [s]) if m is not None else ([], [])
+                m, s = merge(old_parts[0] + tops[:done], old_parts[1] + sums)
+                tops, sums = tops[done:], []
         top = jnp.max(m, axis=0, keepdims=True)
         total = jnp.sum(s * jnp.exp2((m - top) * LOG2E), axis=0, keepdims=True)
         for t in range(2):
@@ -262,8 +274,7 @@
     drain(lab_all.at[pl.ds(0, n - 1)], lab_sem.at[1])
     swap_q = swap_cores(q_all, swap_sem)
 
-    @pl.loop(0, BLOCKS)
-    def _(k):
+    def grads(k, kept):
         send_rows(BLOCKS + k)
 
         @pl.when(k == BLOCKS - 1)
@@ -285,43 +296,31 @@
         dxt[...] = jnp.zeros_like(dxt)
         gb[...] = jnp.zeros_like(gb)
 
-        zb[...] = jnp.full((SUB, QB), LOW, F32)
-        ga[...] = jnp.zeros_like(ga)
 
         def spread(src, dst, q):
-            at = lab - jnp.where(q < 0, -(1 << 29), q * SUB)
-            at = jnp.broadcast_to(at, (8, QB))
             tsum = t_acc[...]
-            for u in range(SUB // 16):
-                parts = []
-                for v in range(2):
-                    rows8 = pl.ds(u * 16 + v * 8, 8)
-                    z = src[rows8, :]
-                    idv = ids[rows8, :]
-                    hot = jnp.where(jnp.concatenate([idv, idv], axis=1) == at, 1.0 / (n * rows), 0.0)
-                    tsum = tsum + z * hot
-                    parts.append(jnp.exp2(z * LOG2E) - hot)
-                dst[u * 16:(u + 1) * 16, :] = jnp.concatenate(parts, axis=0).astype(BF16)
+            for u in range(SUB // 64):
+                part = pl.ds(u * 64, 64)
+                z = src[part, :]
+                idv = ids[part, :]
+                hot = jnp.where(jnp.concatenate([idv, idv], axis=1) == lab - q * SUB, 1.0 / (n * rows), 0.0)
+                tsum = tsum + jnp.sum((z * hot).reshape(8, 8, QB), axis=0)
+                dst[part, :] = (jnp.exp2(z * LOG2E) - hot).astype(BF16)
             t_acc[...] = tsum
 
-        def gather(src, q):
-            r = pl.ds(pl.multiple_of(jnp.maximum(q, 0) * SUB, SUB), SUB)
-            de_acc[r, :] += jnp.dot(src[...], xb[...], preferred_element_type=F32)
-            dxt[...] += jnp.dot(et[:, r], src[...], preferred_element_type=F32)
-
-        @pl.loop(0, chunks // UNROLL)
-        def _(i):
-            for u in range(UNROLL):
-                q = i * UNROLL + u
-                new, old = (za, zb) if u % 2 == 0 else (zb, za)
-                here, gone = (gb, ga) if u % 2 == 0 else (ga, gb)
-                new[...] = logits(q)
-                spread(old, here, q - 1)
-                gather(gone, q - 2)
-
-        spread(zb, gb, chunks - 1)
-        gather(ga, chunks - 2)
-        gather(gb, chunks - 1)
+        for q in range(chunks + 2):
+            if q < chunks:
+                (za if q % 2 == 0 else zb)[...] = logits(q)
+            if 0 < q <= chunks:
+                to = ga if q % 2 else gb
+                spread(zb if q % 2 == 0 else za, to if kept is None else keep.at[kept, pl.ds((q - 1) * SUB, SUB)], q - 1)
+            if q > 1:
+                r = pl.ds((q - 2) * SUB, SUB)
+                g = (gb if q % 2 else ga)[...] if kept is None else keep[kept, r, :]
+                if kept is None:
+                    de_acc[r, :] += jnp.dot(g, xb[...], preferred_element_type=F32)
+                dxt[...] += jnp.dot(et[:, r], g, preferred_element_type=F32)
+
         dx_part[pl.ds(k * ob, ob)] = dxt[...].T.reshape(ob, rows, 128)
 
         pltpu.make_async_remote_copy(dx_part.at[pl.ds(k * ob + (1 - core) * half, half)], pair.at[pl.ds(k * half, half)], pair_send, pair_recv.at[k],
@@ -335,19 +334,27 @@
 
         combine_rows(k - 3)
 
+    pl.loop(0, BLOCKS - KEEP)(lambda k: grads(k, None))
+    pl.loop(BLOCKS - KEEP, BLOCKS)(lambda k: grads(k, k - (BLOCKS - KEEP)))
+
     t_mine[...] = jnp.sum(t_acc[:, 0:128] + t_acc[:, 128:256], axis=0, keepdims=True)
     t_all[pl.ds(me, 1)] = t_mine[...][None]
 
-    @pl.loop(1, n)
-    def _(i):
+    def send_t(i):
         pltpu.make_async_remote_copy(t_mine, t_all.at[me], t_sem.at[0], t_sem.at[1], device_id=peer(lax.rem(me + i, n)), device_id_type=MESH).start()
 
+    each(1, n, send_t)
+
     flush(BLOCKS - 1)
+
+    for i in range(KEEP):
+        xk[pl.ds(i * QB, QB), :] = x_all[pl.ds(row0(BLOCKS - KEEP + i), ob)].reshape(QB, 128)
 
     @pl.loop(0, items // 512)
     def _(i):
-        r = pl.multiple_of(i * 512, 512)
-        de_out[pl.ds(r, 512), :] = de_acc[pl.ds(r, 512), :].astype(BF16)
+        r = pl.ds(pl.multiple_of(i * 512, 512), 512)
+        g = jnp.concatenate([keep[b, r, :] for b in range(KEEP)], axis=1)
+        de_out[r, :] = (de_acc[r, :] + jnp.dot(g, xk[...], preferred_element_type=F32)).astype(BF16)
 
     out = pltpu.make_async_copy(de_out, de_hbm, out_sem)
     out.start()
@@ -471,7 +478,7 @@
             out_specs=(pl.BlockSpec(memory_space=pltpu.SMEM), ANY, V, V),
             scratch_shapes=[
                 M((width, hidden), BF16), M((hidden, 128), BF16), M((items, 256), BF16), M((128, items), BF16), M((SUB, 128), i32),
-                M((rows, 128), BF16), M((1, 128), i32), M((n, rows, 128), BF16), M((n, 1, 128), i32), M((n, rows, width), BF16), M((256, QB), BF16), M((QB, 128), BF16), M((SUB, QB), F32), M((SUB, QB), F32), M((SUB, QB), BF16), M((SUB, QB), BF16),
+                M((rows, 128), BF16), M((1, 128), i32), M((n, rows, 128), BF16), M((n, 1, 128), i32), M((n, rows, width), BF16), M((256, QB), BF16), M((QB, 128), BF16), M((SUB, QB), F32), M((SUB, QB), F32), M((SUB, QB), BF16), M((SUB, QB), BF16), M((KEEP, items, QB), BF16), M((KEEP * QB, 128), BF16),
                 M((2 * BLOCKS, 2, 128), F32), M((n, 2, 128), F32), M((2, 128), F32), M((2 * BLOCKS, 2, 128), F32), M((items, 128), F32), M((items, 128), BF16), M((128, QB), F32),
                 M((n, rows, 128), F32), M((n // 2, rows, 128), F32), M((n // 2, rows, 128), F32), M((n // 2, rows, 128), F32), M((rows, 128), BF16), M((n, rows, 128), BF16),
                 M((8, QB), F32), M((1, 128), F32), M((n, 1, 128), F32), M((BLOCKS, QB, hidden), F32), M((width, hidden), F32), M((hidden, 128), F32),

time: 96.3 us -> 97 us (level)
  no operation moved by 1% of the time
where the time goes in v6:
time: 97 us; the launch traced here: 96.6 us
  Pallas kernels  94.1 us (97%)
  between operations  2.41 us (2%)
    pallas_call x1, Pallas kernels, local_step(): pl.pallas_call(functools.partial(kernel, n, rows, items), name='two_tower...  91.2 us
    pallas_call x1, Pallas kernels, store(): pl.pallas_call(functools.partial(store_kernel, pieces), name='store', out...  2.92 us

profile of v6, /device:TPU:1, one launch (start us, length us, event | category | flops | bytes accessed | tf_op | source)
XLA Modules:
  0.0 96.6 jit_solution(13793897989935116757)
XLA Ops:
  0.6 91.2 %two_tower.1 = (f32[1]{0:T(128)}, bf16[8192,128]{1,0:T(8,128)(2,1)}, bf16[768,768]{1,0:T(8,128)(2,1)}, bf16[768,128]{1,0:T(8,128)(2,1)}) custom-call(bf16[16,768]{1,0:T(8,128)(2,1)} %q_ref.1, bf16[768,768]{1,0:T(8,128)(2,1)} %w1_hbm.1, bf16[768,128]{1,0:T(8,128)(2,1)} %w2_hbm.1, bf16[8192,128]{1,0:T(8,128)(2,1)} %e_hbm.1, f32[64,128]{1,0:T(8,128)} %bitcast.2, ...), custom_call_target="tpu_custom_call" | custom-call | tf_op jit(solution)/shard_map/two_tower/pallas_call | solution.py:473
  91.9 2.9 %store.1 = (bf16[8192,128]{1,0:T(8,128)(2,1)}, bf16[768,768]{1,0:T(8,128)(2,1)}, bf16[768,128]{1,0:T(8,128)(2,1)}) custom-call(bf16[8192,128]{1,0:T(8,128)(2,1)} %get-tuple-element.12.refs_0_, bf16[768,768]{1,0:T(8,128)(2,1)} %get-tuple-element.13.refs_1_, bf16[768,128]{1,0:T(8,128)(2,1)} %get-tuple-element.14.refs_2_), custom_call_target="tpu_custom_call" | custom-call | tf_op jit(solution)/shard_map/store/pallas_call | solution.py:450

commit v7 on v6

--- a/solution.py
+++ b/solution.py
@@ -14,7 +14,7 @@
 BLOCKS = 8
 QB = 256
 SUB = 512
-KEEP = 3
+KEEP = 1
 
 
 def peer(index):
@@ -277,11 +277,6 @@
     def grads(k, kept):
         send_rows(BLOCKS + k)
 
-        @pl.when(k == BLOCKS - 1)
-        def _():
-            drain(q_all.at[pl.ds(0, chips - 1)], q_sem.at[1])
-            swap_q.start()
-
         for t in range(2):
             @pl.when(stat_owner(k, t, n) != me)
             def _():
@@ -332,7 +327,7 @@
 
         combine_stats(k + 3)
 
-        combine_rows(k - 3)
+        combine_rows(k - 4)
 
     pl.loop(0, BLOCKS - KEEP)(lambda k: grads(k, None))
     pl.loop(BLOCKS - KEEP, BLOCKS)(lambda k: grads(k, k - (BLOCKS - KEEP)))
@@ -346,6 +341,8 @@
     each(1, n, send_t)
 
     flush(BLOCKS - 1)
+    drain(q_all.at[pl.ds(0, chips - 1)], q_sem.at[1])
+    swap_q.start()
 
     for i in range(KEEP):
         xk[pl.ds(i * QB, QB), :] = x_all[pl.ds(row0(BLOCKS - KEEP + i), ob)].reshape(QB, 128)
@@ -358,13 +355,14 @@
 
     out = pltpu.make_async_copy(de_out, de_hbm, out_sem)
     out.start()
+    combine_rows(BLOCKS - 4)
+    combine_rows(BLOCKS - 3)
     drain(q_all.at[pl.ds(0, chips)], swap_sem.at[1])
 
     def rows_of(k):
         return q_all[pl.ds(row0(k), ob)].reshape(QB, q_all.shape[-1])
 
-    @pl.loop(0, BLOCKS)
-    def _(k):
+    def pre_act(k):
         pre[pl.ds(k, 1)] = jnp.dot(rows_of(k), w1[...], preferred_element_type=F32)[None]
 
     def tower(k):
@@ -385,9 +383,10 @@
         da = jnp.where(a > 0.0, dh, 0.0).astype(BF16)
         acc1[...] += lax.dot_general(rows_of(k), da, (((0,), (0,)), ((), ())), preferred_element_type=F32)
 
-    combine_rows(BLOCKS - 3)
+    pl.loop(0, 4)(pre_act)
     combine_rows(BLOCKS - 2)
     combine_rows(BLOCKS - 1)
+    pl.loop(4, BLOCKS)(pre_act)
     pl.loop(0, BLOCKS)(tower)
     dw1_ref[...] = acc1[...].astype(BF16)
     dw2_ref[...] = acc2[...].astype(BF16)

time: 97 us -> 95.8 us (0.988)
  Pallas kernels: 94.1 us -> 93.1 us
    pallas_call x1, Pallas kernels: 91.2 us -> 90.2 us  [local_step(): pl.pallas_call(functools.partial(kernel, n, rows, items), name='two_tower...]
where the time goes in v7:
time: 95.8 us; the launch traced here: 95.5 us
  Pallas kernels  93.1 us (97%)
  between operations  2.41 us (3%)
    pallas_call x1, Pallas kernels, local_step(): pl.pallas_call(functools.partial(kernel, n, rows, items), name='two_tower...  90.2 us
    pallas_call x1, Pallas kernels, store(): pl.pallas_call(functools.partial(store_kernel, pieces), name='store', out...  2.92 us

profile of v7, /device:TPU:1, one launch (start us, length us, event | category | flops | bytes accessed | tf_op | source)
XLA Modules:
  0.0 95.5 jit_solution(233296174532803841)
XLA Ops:
  0.6 90.2 %two_tower.1 = (f32[1]{0:T(128)}, bf16[8192,128]{1,0:T(8,128)(2,1)}, bf16[768,768]{1,0:T(8,128)(2,1)}, bf16[768,128]{1,0:T(8,128)(2,1)}) custom-call(bf16[16,768]{1,0:T(8,128)(2,1)} %q_ref.1, bf16[768,768]{1,0:T(8,128)(2,1)} %w1_hbm.1, bf16[768,128]{1,0:T(8,128)(2,1)} %w2_hbm.1, bf16[8192,128]{1,0:T(8,128)(2,1)} %e_hbm.1, f32[64,128]{1,0:T(8,128)} %bitcast.2, ...), custom_call_target="tpu_custom_call" | custom-call | tf_op jit(solution)/shard_map/two_tower/pallas_call | solution.py:472
  90.8 2.9 %store.1 = (bf16[8192,128]{1,0:T(8,128)(2,1)}, bf16[768,768]{1,0:T(8,128)(2,1)}, bf16[768,128]{1,0:T(8,128)(2,1)}) custom-call(bf16[8192,128]{1,0:T(8,128)(2,1)} %get-tuple-element.12.refs_0_, bf16[768,768]{1,0:T(8,128)(2,1)} %get-tuple-element.13.refs_1_, bf16[768,128]{1,0:T(8,128)(2,1)} %get-tuple-element.14.refs_2_), custom_call_target="tpu_custom_call" | custom-call | tf_op jit(solution)/shard_map/store/pallas_call | solution.py:449

commit v8 on v7

--- a/solution.py
+++ b/solution.py
@@ -220,12 +220,10 @@
             total = total + jnp.sum(jnp.exp2((z - m[None]) * LOG2E), axis=0)
         return total
 
-    per_step = -(-(chips - 1) // (2 * BLOCKS - 2))
-
-    def send_rows(step):
-        @pl.loop(0, per_step)
+    def send_rows(first, count):
+        @pl.loop(0, count)
         def _(i):
-            c = step * per_step + i + 1
+            c = first + i + 1
 
             @pl.when(c < chips)
             def _():
@@ -268,14 +266,16 @@
             def _():
                 st_got[pl.ds(me, 1)] = st_send[pl.ds(k * 2 + t, 1)]
 
-        send_rows(k)
-        combine_stats(jnp.where(k == BLOCKS - 1, 2, jnp.where(k < 6, k - 4, -1)))
+        send_rows(2 * k, 2)
+        combine_stats(k - 4)
 
     drain(lab_all.at[pl.ds(0, n - 1)], lab_sem.at[1])
     swap_q = swap_cores(q_all, swap_sem)
 
+    late = max(-(-(chips - 1 - 2 * BLOCKS) // (BLOCKS - 2)), 1)
+
     def grads(k, kept):
-        send_rows(BLOCKS + k)
+        send_rows(2 * BLOCKS + k * late, late)
 
         for t in range(2):
             @pl.when(stat_owner(k, t, n) != me)
@@ -325,7 +325,7 @@
         def _():
             flush(k - 1)
 
-        combine_stats(k + 3)
+        combine_stats(k + 4)
 
         combine_rows(k - 4)
 
@@ -383,10 +383,10 @@
         da = jnp.where(a > 0.0, dh, 0.0).astype(BF16)
         acc1[...] += lax.dot_general(rows_of(k), da, (((0,), (0,)), ((), ())), preferred_element_type=F32)
 
-    pl.loop(0, 4)(pre_act)
+    pl.loop(0, 2)(pre_act)
     combine_rows(BLOCKS - 2)
     combine_rows(BLOCKS - 1)
-    pl.loop(4, BLOCKS)(pre_act)
+    pl.loop(2, BLOCKS)(pre_act)
     pl.loop(0, BLOCKS)(tower)
     dw1_ref[...] = acc1[...].astype(BF16)
     dw2_ref[...] = acc2[...].astype(BF16)

time: 95.8 us -> 92.3 us (0.963)
  Pallas kernels: 93.1 us -> 89.6 us
    pallas_call x1, Pallas kernels: 90.2 us -> 86.7 us  [local_step(): pl.pallas_call(functools.partial(kernel, n, rows, items), name='two_tower...]
where the time goes in v8:
time: 92.3 us; the launch traced here: 92 us
  Pallas kernels  89.6 us (97%)
  between operations  2.41 us (3%)
    pallas_call x1, Pallas kernels, local_step(): pl.pallas_call(functools.partial(kernel, n, rows, items), name='two_tower...  86.7 us
    pallas_call x1, Pallas kernels, store(): pl.pallas_call(functools.partial(store_kernel, pieces), name='store', out...  2.92 us

profile of v8, /device:TPU:1, one launch (start us, length us, event | category | flops | bytes accessed | tf_op | source)
XLA Modules:
  0.0 92.0 jit_solution(17265159428448801690)
XLA Ops:
  0.6 86.7 %two_tower.1 = (f32[1]{0:T(128)}, bf16[8192,128]{1,0:T(8,128)(2,1)}, bf16[768,768]{1,0:T(8,128)(2,1)}, bf16[768,128]{1,0:T(8,128)(2,1)}) custom-call(bf16[16,768]{1,0:T(8,128)(2,1)} %q_ref.1, bf16[768,768]{1,0:T(8,128)(2,1)} %w1_hbm.1, bf16[768,128]{1,0:T(8,128)(2,1)} %w2_hbm.1, bf16[8192,128]{1,0:T(8,128)(2,1)} %e_hbm.1, f32[64,128]{1,0:T(8,128)} %bitcast.2, ...), custom_call_target="tpu_custom_call" | custom-call | tf_op jit(solution)/shard_map/two_tower/pallas_call | solution.py:472
  87.3 2.9 %store.1 = (bf16[8192,128]{1,0:T(8,128)(2,1)}, bf16[768,768]{1,0:T(8,128)(2,1)}, bf16[768,128]{1,0:T(8,128)(2,1)}) custom-call(bf16[8192,128]{1,0:T(8,128)(2,1)} %get-tuple-element.12.refs_0_, bf16[768,768]{1,0:T(8,128)(2,1)} %get-tuple-element.13.refs_1_, bf16[768,128]{1,0:T(8,128)(2,1)} %get-tuple-element.14.refs_2_), custom_call_target="tpu_custom_call" | custom-call | tf_op jit(solution)/shard_map/store/pallas_call | solution.py:449
